TPU v7x, 128 devices: a whole 4x4x4 slice. The times are simulated.
128 devices in a mesh: gx: 16 (over x, z), gy: 4 (over y), gz: 2 (over core).
Axes of the slice: x: 4, y: 4, z: 4, core: 2. Of those that a mesh axis runs over, the one named last changes fastest.
Arguments:
- u_old: float32 [3, 128, 32, 256], P(None, 'gx', 'gy', 'gz'), may hold values from -1.2 to 1.2
- u_trial: float32 [3, 128, 32, 256], P(None, 'gx', 'gy', 'gz'), may hold values from -3.6 to 3.6
- jacobian_inverse: float32 [3, 3, 128, 32, 256], P(None, None, 'gx', 'gy', 'gz'), may hold values from -0.6 to 1.5
- tile_base: int32 [8192], P(('gx', 'gy', 'gz')), may hold values from 0 to 63
- pair_codes: int32 [4, 8192, 128], P(None, ('gx', 'gy', 'gz')), may hold values from 0 to 127, as said below
- pair_groups: int32 [8192, 128], P(('gx', 'gy', 'gz')), may hold values from 0 to 2, as said below
Outputs:
- u_final: float32 [3, 128, 32, 256], P(None, 'gx', 'gy', 'gz')
- residual_norms: float32 [3], replicated
Inputs may be any that keep to these rules, and one draw needn't show every extreme that they name: `pair_groups`: on each device the tiles that hold a nonempty slot come first, and their first slot is never empty; every slot of the later tiles is 2. A device holds between 16 and 64 such tiles, and some device holds 64. `pair_codes`: Rows: first node 0 to 127, second direction 0 to 5, third offset 0 to 26, fourth direction 0 to 5; every node of a pair lies in the device's cells extended by one cell on every side.
All inputs are finite; a program needn't handle non-finite values.
Results may differ from a plain program's by a relative error of at most 0.0003.
Values sent between devices are 32-bit elements; how exact they have to be, the bound alone decides.
A program may use at most 64 MiB of HBM per device.

v0:
```python
import jax
import jax.numpy as jnp
from jax import lax
from jax.sharding import Mesh
from jax.sharding import PartitionSpec as P

ITERS = 3
GX = ("gx_0", "gx_1")
GX_GY_GZ = ("gx_0", "gx_1", "gy", "gz")


step_size = 0.5
stiffness = 0.5
core_square = 0.5


def shifted(shard, axis, by):
    count = lax.axis_size(axis)
    pairs = [(i, i + by) for i in range(count) if 0 <= i + by < count]
    return lax.ppermute(shard, axis, pairs)


def padded_2(block, sides, width):
    for axis, dim in sides:
        count = lax.axis_size(axis)
        forward = [(i, i + 1) for i in range(count - 1)]
        backward = [(target, source) for source, target in forward]
        low = lax.ppermute(
            lax.slice_in_dim(block, block.shape[dim] - width, None, axis=dim), axis, forward
        )
        high = lax.ppermute(lax.slice_in_dim(block, 0, width, axis=dim), axis, backward)
        block = jnp.concatenate([low, block, high], axis=dim)
    return block


def over_axes(shard, axes):
    for axis in axes:
        shard = lax.psum(shard, axis)
    return shard


def unit_step(step_code):
    which_axis = step_code // 2
    direction = 1 - 2 * (step_code % 2)
    return [jnp.where(which_axis == k, direction, 0) for k in range(3)]


def pair_cells(tile_anchor, pair_code, blocks_y, blocks_z):
    anchor = tile_anchor[:, None]
    block_x = anchor // (blocks_y * blocks_z)
    block_y = anchor // blocks_z % blocks_y
    block_z = anchor % blocks_z
    inside = pair_code[0]
    first_node = [
        block_x * 4 + inside // 32 + 1,
        block_y * 4 + inside // 8 % 4 + 1,
        block_z * 8 + inside % 8 + 1,
    ]
    along_step = unit_step(pair_code[1])
    second_node = [first_node[k] + along_step[k] for k in range(3)]
    offset = pair_code[2]
    third_node = [
        first_node[0] + offset // 9 - 1,
        first_node[1] + offset // 3 % 3 - 1,
        first_node[2] + offset % 3 - 1,
    ]
    across_step = unit_step(pair_code[3])
    fourth_node = [third_node[k] + across_step[k] for k in range(3)]
    return [first_node, second_node, third_node, fourth_node]


def pair_terms(flat_u, node_cells, groups, frozen_too, flat_fn):
    points = []
    for node_cell in node_cells:
        lattice = jnp.stack(node_cell).astype(jnp.float32)
        points.append(lattice + flat_u[:, flat_fn(node_cell)])
    line_one = points[1] - points[0]
    line_two = points[3] - points[2]
    separation = 0.5 * (points[2] + points[3]) - 0.5 * (points[0] + points[1])
    square = jnp.sum(separation * separation, 0) + core_square
    coupling = stiffness * jnp.sum(line_one * line_two, 0) / (square * jnp.sqrt(square))
    push_force = coupling * separation
    pieces = [push_force * (groups == 0).astype(jnp.float32)]
    if frozen_too:
        pieces.append(push_force * (groups == 1).astype(jnp.float32))
    halves = 0.5 * jnp.concatenate(pieces, 0)
    return jnp.concatenate([-halves, -halves, halves, halves], 1)


def fold_back(summed):
    lower_face = shifted(summed[:, 0], GX, -1)
    upper_face = shifted(summed[:, -1], GX, 1)
    summed = summed[:, 1:-1].at[:, -1].add(lower_face).at[:, 0].add(upper_face)
    lower_face = shifted(summed[:, :, 0], "gy", -1)
    upper_face = shifted(summed[:, :, -1], "gy", 1)
    summed = summed[:, :, 1:-1].at[:, :, -1].add(lower_face).at[:, :, 0].add(upper_face)
    lower_face = shifted(summed[:, :, :, 0], "gz", -1)
    upper_face = shifted(summed[:, :, :, -1], "gz", 1)
    return summed[:, :, :, 1:-1].at[:, :, :, -1].add(lower_face).at[:, :, :, 0].add(upper_face)


def per_device(u_old, u_trial, jacobian_inverse, tile_base, pair_codes, pair_groups):
    size_x = u_old.shape[1]
    size_y = u_old.shape[2]
    size_z = u_old.shape[3]
    tile_count = tile_base.shape[0]
    per_block = max(1, tile_count // 16)
    blocks_y = size_y // 4
    blocks_z = size_z // 8
    width_y = size_y + 2
    width_z = size_z + 2
    cell_total = (
        3.0
        * size_x
        * size_y
        * size_z
        * lax.axis_size(GX)
        * lax.axis_size("gy")
        * lax.axis_size("gz")
    )
    live_tiles = jnp.sum(jnp.any(pair_groups < 2, axis=1).astype(jnp.int32))

    def flat_fn(node_cell):
        return (node_cell[0] * width_y + node_cell[1]) * width_z + node_cell[2]

    def accumulate(padded, tile_anchor, pair_code, groups, tile_live, frozen_too):
        flat_u = padded.reshape(3, -1)
        channels = 6 if frozen_too else 3
        tile_index = lax.broadcasted_iota(jnp.int32, groups.shape, 0)
        groups = jnp.where(tile_index < tile_live, groups, 2)

        def one_block(block_turn, summed):
            begin_at = block_turn * per_block
            anchor_part = lax.dynamic_slice_in_dim(tile_anchor, begin_at, per_block, 0)
            code_part = lax.dynamic_slice_in_dim(pair_code, begin_at, per_block, 1)
            group_part = lax.dynamic_slice_in_dim(groups, begin_at, per_block, 0)
            node_cells = pair_cells(anchor_part, code_part, blocks_y, blocks_z)
            values = pair_terms(flat_u, node_cells, group_part, frozen_too, flat_fn)
            flat_index = jnp.concatenate([flat_fn(node_cell) for node_cell in node_cells], 0)
            return summed.at[:, flat_index.reshape(-1)].add(values.reshape(channels, -1))

        block_turns = (tile_live + per_block - 1) // per_block
        initial = jnp.zeros((channels, flat_u.shape[1]), jnp.float32)
        summed = lax.fori_loop(0, block_turns, one_block, initial)
        return summed.reshape(channels, size_x + 2, width_y, width_z)

    def forces(current, frozen_too):
        padded = padded_2(current, ((GX, 1), ("gy", 2), ("gz", 3)), 1)
        summed = accumulate(padded, tile_base, pair_codes, pair_groups, live_tiles, frozen_too)
        return fold_back(summed)

    current = u_trial
    all_forces = forces(current, True)
    frozen = all_forces[3:]
    force_sum = all_forces[:3] + frozen
    square_list = []
    for iteration in range(ITERS):
        if iteration > 0:
            force_sum = forces(current, False) + frozen
        residual = current - u_old - step_size * force_sum
        local_square = jnp.sum(residual * residual)
        square_list.append(local_square)
        applied = [sum((jacobian_inverse[r, m] * residual[m] for m in range(3))) for r in range(3)]
        current = current - jnp.stack(applied)
    squares_all = over_axes(jnp.stack(square_list), GX_GY_GZ)
    residual_norms = jnp.sqrt(squares_all / cell_total)
    return (current, residual_norms)


def solution(mesh):
    finer = Mesh(
        mesh.devices.reshape(4, 4, mesh.shape["gy"], mesh.shape["gz"]), ("gx_0", "gx_1", "gy", "gz")
    )
    in_specs = (
        P(None, GX, "gy", "gz"),
        P(None, GX, "gy", "gz"),
        P(None, None, GX, "gy", "gz"),
        P(GX_GY_GZ),
        P(None, GX_GY_GZ, None),
        P(GX_GY_GZ, None),
    )
    out_specs = (P(None, GX, "gy", "gz"), P())
    return jax.shard_map(
        per_device, mesh=finer, in_specs=in_specs, out_specs=out_specs, check_vma=False
    )
```

profile of v0, /device:TPU:1, one launch (start us, length us, event | category | flops | bytes accessed | tf_op | source)
XLA Modules:
  0.0 1832.0 jit_solution(9042387024011809964)
XLA Ops:
  34.3 234.0 %while.57 = (s32[]{:T(128)}, f32[6,13000]{0,1:T(8,128)}, s32[]{:T(128)}, s32[64]{0:T(128)S(1)}, s32[4,64,128]{2,1,0:T(8,128)S(1)}, /*index=5*/f32[3,13000]{0,1:T...) while((s32[]{:T(128)}, f32[6,13000]{0,1:T(8,128)}, ...), condition=%wide.region_6.7_spmd, body=%wide.region_2.6_spmd.sunk | while | flops 417477 | bytes 766047 | solution.py:144
  51.7 16.0 scatter_fusion
  118.5 16.0 scatter_fusion
  152.0 16.0 scatter_fusion
  185.4 16.0 scatter_fusion
  218.8 16.0 scatter_fusion
  252.2 16.0 scatter_fusion
  274.8 271.5 %collective-permute-start.7 = (f32[6,10,130]{2,1,0:T(8,128)S(1)}, f32[6,10,130]{2,1,0:T(8,128)S(1)}, u32[]{:S(2)}, u32[]{:S(2)}) collective-permute-start(f32[6,10,130]{2,1,0:T(8,128)S(1)} %get-tuple-element.944), channel_id=1, source_target_pairs={{0,8},{8,16},{16,24},{24,32},{32,40},{40,48},{48,56},{56,64},{64,7... | collective-permute-start | bytes 93608 | tf_op jit(solution)/shard_map/ppermute | solution.py:20
  599.9 233.8 %while.58 = (s32[]{:T(128)}, f32[3,13000]{0,1:T(8,128)}, s32[]{:T(128)}, s32[64]{0:T(128)S(1)}, s32[4,64,128]{2,1,0:T(8,128)S(1)}, /*index=5*/f32[3,13000]{0,1:T...) while((s32[]{:T(128)}, f32[3,13000]{0,1:T(8,128)}, ...), condition=%wide.region_11.12_spmd, body=%wide.region_7.11_spmd.sunk | while | flops 384197 | bytes 565343 | solution.py:144
  617.2 16.0 scatter_fusion.1
  650.6 16.0 scatter_fusion.1
  717.4 16.0 scatter_fusion.1
  750.8 16.0 scatter_fusion.1
  817.6 16.0 scatter_fusion.1
  839.9 273.6 %collective-permute-start.19 = (f32[3,10,130]{2,1,0:T(8,128)S(1)}, f32[3,10,130]{2,1,0:T(8,128)S(1)}, u32[]{:S(2)}, u32[]{:S(2)}) collective-permute-start(f32[3,10,130]{2,1,0:T(8,128)S(1)} %get-tuple-element.951), channel_id=1, source_target_pairs={{0,8},{8,16},{16,24},{24,32},{32,40},{40,48},{48,56},{56,64},{64,7... | collective-permute-start | bytes 46808 | tf_op jit(solution)/shard_map/ppermute | solution.py:20
  1137.0 35.3 %collective-permute-start.26 = (f32[3,10,1,128]{3,2,1,0:T(1,128)S(1)}, f32[3,10,1,128]{3,2,1,0:T(1,128)S(1)}, u32[]{:S(2)}, u32[]{:S(2)}) collective-permute-start(f32[3,10,1,128]{3,2,1,0:T(1,128)S(1)} %get-tuple-element.972), channel_id=1, source_target_pairs={{0,2},{2,4},{4,6},{1,3},{3,5},{5,7},{8,10},{10,12},{12,14},{9,11},... | collective-permute-start | bytes 46088 | tf_op jit(solution)/shard_map/ppermute | solution.py:28
  1192.3 233.8 %while.59 = (s32[]{:T(128)}, f32[3,13000]{0,1:T(8,128)}, s32[]{:T(128)}, s32[64]{0:T(128)S(1)}, s32[4,64,128]{2,1,0:T(8,128)S(1)}, /*index=5*/f32[3,13000]{0,1:T...) while((s32[]{:T(128)}, f32[3,13000]{0,1:T(8,128)}, ...), condition=%wide.region_16.17_spmd, body=%wide.region_12.16_spmd.sunk | while | flops 384197 | bytes 565343 | solution.py:144
  1209.6 16.0 scatter_fusion.2
  1243.0 16.0 scatter_fusion.2
  1309.8 16.0 scatter_fusion.2
  1343.2 16.0 scatter_fusion.2
  1410.0 16.0 scatter_fusion.2
  1432.3 273.6 %collective-permute-start.31 = (f32[3,10,130]{2,1,0:T(8,128)S(1)}, f32[3,10,130]{2,1,0:T(8,128)S(1)}, u32[]{:S(2)}, u32[]{:S(2)}) collective-permute-start(f32[3,10,130]{2,1,0:T(8,128)S(1)} %get-tuple-element.949), channel_id=1, source_target_pairs={{0,8},{8,16},{16,24},{24,32},{32,40},{40,48},{48,56},{56,64},{64,7... | collective-permute-start | bytes 46808 | tf_op jit(solution)/shard_map/ppermute | solution.py:20
  1723.0 75.4 %psum.28 = f32[3]{0:T(128)S(1)} all-reduce(f32[3]{0:T(128)S(1)} %pad_maximum_fusion.15), channel_id=1, replica_groups=mesh['gx_0'=4,'gx_1'=4,'gy'=4,'gz'=2] {'gx_0'}, use_global_device_ids=true, to_apply=%region_20.21 | all-reduce | flops 3 | bytes 24 | tf_op jit(solution)/shard_map/psum | solution.py:38
  (811 shorter events, 641.6 us)
Async XLA Ops:
  1.4 7.2 collective-permute-start
  10.4 5.2 collective-permute-start.2
  18.2 8.1 collective-permute-start.4
  19.5 6.8 collective-permute-start.5
  273.5 272.9 %collective-permute-start.6 = (f32[6,10,130]{2,1,0:T(8,128)S(1)}, f32[6,10,130]{2,1,0:T(8,128)S(1)}, u32[]{:S(2)}, u32[]{:S(2)}) collective-permute-start(f32[6,10,130]{2,1,0:T(8,128)S(1)} %get-tuple-element.945), channel_id=1, source_target_pairs={{8,0},{16,8},{24,16},{32,24},{40,32},{48,40},{56,48},{64,56},{72,6... | collective-permute-start | bytes 93608 | tf_op jit(solution)/shard_map/ppermute | solution.py:20
  274.8 273.2 %collective-permute-start.7 = (f32[6,10,130]{2,1,0:T(8,128)S(1)}, f32[6,10,130]{2,1,0:T(8,128)S(1)}, u32[]{:S(2)}, u32[]{:S(2)}) collective-permute-start(f32[6,10,130]{2,1,0:T(8,128)S(1)} %get-tuple-element.944), channel_id=1, source_target_pairs={{0,8},{8,16},{16,24},{24,32},{32,40},{40,48},{48,56},{56,64},{64,7... | collective-permute-start | bytes 93608 | tf_op jit(solution)/shard_map/ppermute | solution.py:20
  548.1 5.4 collective-permute-start.8
  549.5 6.2 collective-permute-start.9
  567.5 5.0 collective-permute-start.12
  575.7 5.8 collective-permute-start.14
  585.1 5.9 collective-permute-start.16
  586.4 5.5 collective-permute-start.17
  838.6 274.9 %collective-permute-start.18 = (f32[3,10,130]{2,1,0:T(8,128)S(1)}, f32[3,10,130]{2,1,0:T(8,128)S(1)}, u32[]{:S(2)}, u32[]{:S(2)}) collective-permute-start(f32[3,10,130]{2,1,0:T(8,128)S(1)} %get-tuple-element.952), channel_id=1, source_target_pairs={{8,0},{16,8},{24,16},{32,24},{40,32},{48,40},{56,48},{64,56},{72,6... | collective-permute-start | bytes 46808 | tf_op jit(solution)/shard_map/ppermute | solution.py:20
  839.9 274.7 %collective-permute-start.19 = (f32[3,10,130]{2,1,0:T(8,128)S(1)}, f32[3,10,130]{2,1,0:T(8,128)S(1)}, u32[]{:S(2)}, u32[]{:S(2)}) collective-permute-start(f32[3,10,130]{2,1,0:T(8,128)S(1)} %get-tuple-element.951), channel_id=1, source_target_pairs={{0,8},{8,16},{16,24},{24,32},{32,40},{40,48},{48,56},{56,64},{64,7... | collective-permute-start | bytes 46808 | tf_op jit(solution)/shard_map/ppermute | solution.py:20
  1114.7 5.3 collective-permute-start.20
  1128.8 5.0 collective-permute-start.24
  1137.0 36.6 %collective-permute-start.26 = (f32[3,10,1,128]{3,2,1,0:T(1,128)S(1)}, f32[3,10,1,128]{3,2,1,0:T(1,128)S(1)}, u32[]{:S(2)}, u32[]{:S(2)}) collective-permute-start(f32[3,10,1,128]{3,2,1,0:T(1,128)S(1)} %get-tuple-element.972), channel_id=1, source_target_pairs={{0,2},{2,4},{4,6},{1,3},{3,5},{5,7},{8,10},{10,12},{12,14},{9,11},... | collective-permute-start | bytes 46088 | tf_op jit(solution)/shard_map/ppermute | solution.py:28
  1172.3 5.0 collective-permute-start.27
  1177.5 5.7 collective-permute-start.28
  1178.8 5.5 collective-permute-start.29
  1431.0 274.9 %collective-permute-start.30 = (f32[3,10,130]{2,1,0:T(8,128)S(1)}, f32[3,10,130]{2,1,0:T(8,128)S(1)}, u32[]{:S(2)}, u32[]{:S(2)}) collective-permute-start(f32[3,10,130]{2,1,0:T(8,128)S(1)} %get-tuple-element.950), channel_id=1, source_target_pairs={{8,0},{16,8},{24,16},{32,24},{40,32},{48,40},{56,48},{64,56},{72,6... | collective-permute-start | bytes 46808 | tf_op jit(solution)/shard_map/ppermute | solution.py:20
  1432.3 274.7 %collective-permute-start.31 = (f32[3,10,130]{2,1,0:T(8,128)S(1)}, f32[3,10,130]{2,1,0:T(8,128)S(1)}, u32[]{:S(2)}, u32[]{:S(2)}) collective-permute-start(f32[3,10,130]{2,1,0:T(8,128)S(1)} %get-tuple-element.949), channel_id=1, source_target_pairs={{0,8},{8,16},{16,24},{24,32},{32,40},{40,48},{48,56},{56,64},{64,7... | collective-permute-start | bytes 46808 | tf_op jit(solution)/shard_map/ppermute | solution.py:20
  1707.1 5.3 collective-permute-start.32
  1708.5 4.9 collective-permute-start.33
  (17 other events, 955.7 us)
where the time goes:
time: 1840 us; the launch traced here: 1830 us
  starting transfers between devices  927 us (50%)
  local copies, waits for them, and re-layouts  401 us (22%)
  other arithmetic  363 us (20%)
  blocking collectives  108 us (6%)
  waiting for transfers between devices  28.7 us (2%)
    ppermute x18, starting transfers between devices, shifted(): return lax.ppermute(shard, axis, pairs)  846 us
    gather x168, local copies, waits for them, and re-layouts, pair_terms(): points.append(lattice + flat_u[:, flat_fn(node_cell)])  339 us
    scatter-add x21, other arithmetic, one_block(): summed.at[:, flat_index.reshape(-1)].add(values.reshape(channels, -1))  337 us
    psum x4, blocking collectives, over_axes(): shard = lax.psum(shard, axis)  108 us
    ppermute x9, starting transfers between devices, padded_2(): lax.ppermute(lax.slice_in_dim(block, block.shape[dim] - width, None, axis...  58.7 us
  transfers between devices with their start and end apart: 36, of which 16 were waited for; matrix products, arithmetic and copies ran while one was open for 0% of the time, Pallas kernels for 0%

commit v1 on v0

v1 whole, which is shorter than its diff:
```python
import functools

import jax
import jax.numpy as jnp
from jax import lax
from jax.experimental import pallas as pl
from jax.experimental.pallas import tpu as pltpu
from jax.sharding import PartitionSpec as P

ITERS = 3
MESH = pl.DeviceIdType.MESH
F32 = jnp.float32
BF16 = jnp.bfloat16
I32 = jnp.int32

DIRS = [
    (dx, dy, z)
    for dx in (-1, 0, 1)
    for dy in (-1, 0, 1)
    for z in (0, 1)
    if (dx, dy, z) != (0, 0, 0)
]


def slot_of(dx, dy, z):
    return ((dx + 1) * 3 + dy + 1) * 2 + z


def iota(shape, dim):
    return lax.broadcasted_iota(I32, shape, dim)


def take(x, idx):
    return jnp.take_along_axis(x, idx, axis=1, mode="promise_in_bounds")


def split(x):
    hi = x.astype(BF16).astype(F32)
    return hi, x - hi


def kernel(
    nx, ny, cells,
    tb_ref, uold, utrial, jac, codes, groups,
    uout, nout,
    uc, uy, rxz, rxx, rxy, rxd,
    pb, pz, yr, frz, frx, fry, frd,
    win, gat, kidx, lidx, geo, frozen, halves, onehot, ohg, ohs, outs, acc,
    sq, ara, arb,
    send_sem, recv_sem, asend, arecv, bsend, brecv,
):
    gx, gy, gz = lax.axis_index("gx"), lax.axis_index("gy"), lax.axis_index("gz")
    tiles = groups.shape[0]
    x_ok = {-1: gx > 0, 0: None, 1: gx < nx - 1}
    y_ok = {-1: gy > 0, 0: None, 1: gy < ny - 1}

    def exists(dx, dy):
        if dx == 0 and dy == 0:
            return None
        if dx == 0:
            return y_ok[dy]
        if dy == 0:
            return x_ok[dx]
        return jnp.logical_and(x_ok[dx], y_ok[dy])

    def guarded(cond, fn):
        if cond is None:
            fn()
        else:
            pl.when(cond)(fn)

    def valid(cond, value):
        return value if cond is None else jnp.where(cond, value, 0.0)

    def target(dx, dy, z):
        return (gx + dx, gy + dy, gz if z == 0 else 1 - gz)

    barrier = pltpu.get_barrier_semaphore()

    def greet(device):
        pl.semaphore_signal(barrier, inc=1, device_id=device, device_id_type=MESH)

    for d in DIRS:
        guarded(exists(d[0], d[1]), functools.partial(greet, target(*d)))
    for o in range(1, 2 * ny):
        greet((gx, lax.rem(gy + o // 2, ny), lax.rem(gz + o, 2)))
    for o in range(1, nx):
        greet((lax.rem(gx + o, nx), gy, gz))

    def lo_hi(d):
        return 1 if d > 0 else 0

    def displacement_message(it, d):
        dx, dy, z = d
        if dx == 0 and dy == 0:
            return uc, rxz.at[it]
        if dy == 0:
            return uc.at[:, 7 * lo_hi(dx)], rxx.at[it, 1 - lo_hi(dx), z]
        if dx == 0:
            return uy.at[lo_hi(dy)], rxy.at[it, 1 - lo_hi(dy), z]
        return uy.at[lo_hi(dy)], rxd.at[it, 1 - lo_hi(dx), 1 - lo_hi(dy), z]

    def force_message(it, d):
        dx, dy, z = d
        if dx == 0 and dy == 0:
            return pz.at[:, 1:9], frz.at[it]
        if dy == 0:
            return (pz if z else pb).at[:, 9 * lo_hi(dx)], frx.at[it, 1 - lo_hi(dx), z]
        if dx == 0:
            return yr.at[z, lo_hi(dy), :, 0:8], fry.at[it, 1 - lo_hi(dy), z]
        return yr.at[z, lo_hi(dy), :, 8:16], frd.at[it, 1 - lo_hi(dx), 1 - lo_hi(dy), z]

    def copy_of(message, it, phase, d):
        src, dst = message(it, d)
        dx, dy, z = d
        return pltpu.make_async_remote_copy(
            src_ref=src,
            dst_ref=dst,
            send_sem=send_sem.at[phase, slot_of(dx, dy, z)],
            recv_sem=recv_sem.at[phase, slot_of(-dx, -dy, z)],
            device_id=target(dx, dy, z),
            device_id_type=MESH,
        )

    def start_all(message, it, phase):
        for d in DIRS:
            guarded(exists(d[0], d[1]), lambda d=d: copy_of(message, it, phase, d).start())

    def wait_all(message, it, phase):
        for d in DIRS:
            back = (-d[0], -d[1], d[2])
            guarded(exists(d[0], d[1]), lambda d=back: copy_of(message, it, phase, d).wait_recv())
        for d in DIRS:
            guarded(exists(d[0], d[1]), lambda d=d: copy_of(message, it, phase, d).wait_send())

    row8 = iota((8, 128), 0)
    lane8 = iota((8, 128), 1)

    def store_row_packs(read):
        for c in range(3):
            for x in range(8):
                plane = read(c, x)
                uy[0, c, x : x + 1, :] = plane[0:1]
                uy[1, c, x : x + 1, :] = plane[7:8]

    lane_k = iota((8, 128), 1)
    for g in range(tiles // 8):
        base = jnp.zeros((8, 128), I32)
        for i in range(8):
            base = jnp.where(row8 == i, tb_ref[g * 8 + i], base)
        s = (base >> 4) & 1
        sz = base & 15
        par = sz & 1
        j = sz >> 1
        sx = base >> 5
        i_of = (16 - j - par) & 7
        turn = j + par + jnp.where(s == 0, -2, 2)
        place = s * 16 + par * 8 + i_of
        ohg[g * 8 : g * 8 + 8, :] = jnp.where(
            jnp.logical_and((lane_k >> 6) == sx, (lane_k & 31) == place), 1.0, 0.0
        )
        ohs[g * 8 : g * 8 + 8, :] = jnp.where(lane_k == sx * 32 + place, 1.0, 0.0)
        q0 = codes[0, g * 8 : g * 8 + 8, :]
        q1 = codes[1, g * 8 : g * 8 + 8, :]
        q2 = codes[2, g * 8 : g * 8 + 8, :]
        q3 = codes[3, g * 8 : g * 8 + 8, :]

        def unit(q):
            sign = 1 - 2 * (q & 1)
            axis = q >> 1
            return [jnp.where(axis == k, sign, 0) for k in range(3)]

        e1, e2 = unit(q1), unit(q3)
        off = [((q2 * 57) >> 9) - 1, 0, 0]
        third = (q2 * 43) >> 7
        off[1] = third - 3 * (off[0] + 1) - 1
        off[2] = q2 - 3 * third - 1
        first = [(q0 >> 5) + 2, ((q0 >> 3) & 3) + 2, (q0 & 7) + 2]
        nodes = [first, [first[k] + e1[k] for k in range(3)], [first[k] + off[k] for k in range(3)]]
        nodes.append([nodes[2][k] + e2[k] for k in range(3)])
        for n in range(4):
            x, y, z = nodes[n]
            kidx[n, g * 8 : g * 8 + 8, :] = x
            lidx[n, g * 8 : g * 8 + 8, :] = ((y + turn) & 7) * 16 + z
        for k in range(3):
            a, b = e1[k].astype(F32), e2[k].astype(F32)
            geo[k, g * 8 : g * 8 + 8, :] = a
            geo[3 + k, g * 8 : g * 8 + 8, :] = b
            geo[6 + k, g * 8 : g * 8 + 8, :] = off[k].astype(F32) + 0.5 * b - 0.5 * a
    for c in range(3):
        frozen[c] = jnp.zeros((tiles, 128), F32)
    zero_plane = jnp.zeros((64, 384), BF16)
    win[0] = zero_plane
    win[11] = zero_plane

    beside_x = (gx > 0).astype(I32) + (gx < nx - 1).astype(I32)
    beside_y = (gy > 0).astype(I32) + (gy < ny - 1).astype(I32)
    pl.semaphore_wait(barrier, 2 * (1 + beside_x) * (1 + beside_y) - 1 + 2 * ny - 1 + nx - 1)
    uc[...] = utrial[...]
    store_row_packs(lambda c, x: utrial[c, x])
    start_all(displacement_message, 0, 0)

    row128 = iota((128, 128), 0)

    def make_onehot(t, carry):
        for n in range(4):
            row = lidx[n, pl.ds(t, 1), :]
            sign = -1.0 if n < 2 else 1.0
            onehot[t, :, n * 128 : (n + 1) * 128] = jnp.where(row128 == row, sign, 0.0).astype(BF16)
        return carry

    lax.fori_loop(0, tiles, make_onehot, 0)
    pick = ohg[...].astype(BF16)
    spread_t = jnp.transpose(ohs[...])[0:64, 0:tiles].astype(BF16)
    spread = jnp.concatenate([spread_t, spread_t], axis=1)

    group_bits = [((lane8 >> 4) & bit) != 0 for bit in (1, 2, 4)]
    unroll = [(lane8 + 16 * row8 + 2 + 8 * p) & 127 for p in (0, 1)]
    edge_row = {0: row8 == 7, 1: row8 == 0}
    edge_lane = {0: lane8 == 127, 1: lane8 == 0}
    z_ok = {0: gz == 1, 1: gz == 0}
    my_edge_lane = lane8 == jnp.where(gz == 0, 0, 127)

    def iteration(it, carry):
        wait_all(displacement_message, it, 2 * it)

        for x in range(10):
            for c in range(3):
                if 1 <= x <= 8:
                    own, other = uc[c, x - 1], rxz[it, c, x - 1]
                    rows = [
                        [valid(y_ok[dy], rxy[it, lo_hi(dy), z, c, x - 1 : x, :]) for z in (0, 1)]
                        for dy in (-1, 1)
                    ]
                else:
                    dx, xi = (-1, 0) if x == 0 else (1, 1)
                    own = valid(x_ok[dx], rxx[it, xi, 0, c])
                    other = valid(x_ok[dx], rxx[it, xi, 1, c])
                    at = 7 if x == 0 else 0
                    rows = [
                        [
                            valid(exists(dx, dy), rxd[it, xi, lo_hi(dy), z, c, at : at + 1, :])
                            for z in (0, 1)
                        ]
                        for dy in (-1, 1)
                    ]
                for s in range(2):
                    near = jnp.where(edge_row[s], rows[s][0], own)
                    far = jnp.where(edge_row[s], rows[s][1], other)
                    pair = []
                    for p in range(2):
                        source = jnp.where(edge_lane[p], jnp.where(z_ok[p], far, 0.0), near)
                        v = pltpu.roll(source, 2 + 8 * p, axis=1, stride=16, stride_axis=0)
                        for bit, mask in zip((1, 2, 4), group_bits):
                            v = jnp.where(mask, pltpu.roll(v, 8 - bit, axis=0), v)
                        pair.append(v)
                    both = jnp.concatenate(pair, axis=0)
                    hi, lo = split(both)
                    win[x + 1, s * 16 : s * 16 + 16, c * 128 : (c + 1) * 128] = hi.astype(BF16)
                    win[x + 1, 32 + s * 16 : 48 + s * 16, c * 128 : (c + 1) * 128] = lo.astype(BF16)
        for k in range(8):
            both = jnp.concatenate([win[k], win[k + 4]], axis=0)
            gat[k] = jnp.dot(pick, both, preferred_element_type=F32)

        live_below = jnp.where(it == 0, 2, 1)

        def group(g, carry):
            at = pl.ds(pl.multiple_of(g * 8, 8), 8)
            points = []
            for n in range(4):
                ks = kidx[n, at, :]
                ls = lidx[n, at, :]
                least, most = ((2, 5), (1, 6), (1, 6), (0, 7))[n]
                found = []
                for c in range(3):
                    value = take(gat[least, at, c * 128 : (c + 1) * 128], ls)
                    for k in range(least + 1, most + 1):
                        value = jnp.where(ks == k, take(gat[k, at, c * 128 : (c + 1) * 128], ls), value)
                    found.append(value)
                points.append(found)
            one = [points[1][c] - points[0][c] + geo[c, at, :] for c in range(3)]
            two = [points[3][c] - points[2][c] + geo[3 + c, at, :] for c in range(3)]
            apart = [
                0.5 * (points[2][c] + points[3][c]) - 0.5 * (points[0][c] + points[1][c])
                + geo[6 + c, at, :]
                for c in range(3)
            ]
            square = apart[0] * apart[0] + apart[1] * apart[1] + apart[2] * apart[2] + 0.5
            dots = one[0] * two[0] + one[1] * two[1] + one[2] * two[2]
            coupling = 0.5 * dots / (square * jnp.sqrt(square))
            fresh = groups[at, :] < live_below
            for c in range(3):
                force = jnp.where(fresh, coupling * apart[c], frozen[c, at, :])
                frozen[c, at, :] = force
                hi, lo = split(0.5 * force)
                halves[2 * c, at, :] = hi
                halves[2 * c + 1, at, :] = lo
            for i in range(8):
                t = g * 8 + i
                values = [halves[q, pl.ds(t, 1), :] for q in range(6)]
                columns = []
                for n in range(4):
                    mask = row8 == kidx[n, pl.ds(t, 1), :]
                    columns.append(
                        jnp.concatenate([jnp.where(mask, v, 0.0) for v in values], axis=0).astype(BF16)
                    )
                lhs = jnp.concatenate(columns, axis=1)
                got = lax.dot_general(
                    lhs, onehot[t], (((1,), (1,)), ((), ())), preferred_element_type=F32
                )
                for c in range(3):
                    outs[c, pl.ds(pl.multiple_of(t * 8, 8), 8), :] = (
                        got[16 * c : 16 * c + 8] + got[16 * c + 8 : 16 * c + 16]
                    )
            return carry

        lax.fori_loop(0, tiles // 8, group, 0)

        for k in range(8):
            columns = []
            for c in range(3):
                hi, lo = split(outs[c, pl.ds(k, tiles, stride=8), :])
                columns.append(jnp.concatenate([hi, lo], axis=0).astype(BF16))
            acc[k] = jnp.dot(spread, jnp.concatenate(columns, axis=1), preferred_element_type=F32)

        for x in range(10):
            for c in range(3):
                cut = slice(c * 128, (c + 1) * 128)
                parts = []
                for s in range(2):
                    line, beyond = None, None
                    for p in range(2):
                        at = s * 16 + p * 8
                        v = None
                        if x + 1 <= 7:
                            v = acc[x + 1, at : at + 8, cut]
                        if x + 1 >= 4:
                            w = acc[x - 3, 32 + at : 40 + at, cut]
                            v = w if v is None else v + w
                        for bit, mask in zip((1, 2, 4), group_bits):
                            v = jnp.where(mask, pltpu.roll(v, bit, axis=0), v)
                        v = take(v, unroll[p])
                        inside = jnp.where(edge_lane[p], 0.0, v)
                        outside = jnp.where(z_ok[p], v, 0.0)
                        line = inside if line is None else line + inside
                        beyond = outside if beyond is None else beyond + outside
                    parts.append((line, jnp.where(my_edge_lane, beyond, 0.0)))
                row_at = (x + 15) % 16
                for z in range(2):
                    (pz if z else pb)[c, x] = jnp.where(edge_row[0], 0.0, parts[0][z]) + jnp.where(
                        edge_row[1], 0.0, parts[1][z]
                    )
                    yr[z, 0, c, row_at : row_at + 1, :] = parts[0][z][7:8]
                    yr[z, 1, c, row_at : row_at + 1, :] = parts[1][z][0:1]
        start_all(force_message, it, 2 * it + 1)
        wait_all(force_message, it, 2 * it + 1)

        squares = jnp.zeros((8, 128), F32)
        for x in range(8):
            residual = []
            for c in range(3):
                total = pb[c, x + 1] + frz[it, c, x]
                for dx, xe in ((-1, 0), (1, 7)):
                    if x == xe:
                        xi = lo_hi(dx)
                        total = total + valid(x_ok[dx], frx[it, xi, 0, c] + frx[it, xi, 1, c])
                for dy in (-1, 1):
                    yi = lo_hi(dy)
                    line = valid(
                        y_ok[dy], fry[it, yi, 0, c, x : x + 1, :] + fry[it, yi, 1, c, x : x + 1, :]
                    )
                    for dx, xe, rd in ((-1, 0, 0), (1, 7, 7)):
                        if x == xe:
                            xi = lo_hi(dx)
                            line = line + valid(
                                exists(dx, dy),
                                frd[it, xi, yi, 0, c, rd : rd + 1, :] + frd[it, xi, yi, 1, c, rd : rd + 1, :],
                            )
                    total = total + jnp.where(row8 == (0 if dy < 0 else 7), line, 0.0)
                r = uc[c, x] - uold[c, x] - 0.5 * total
                squares = squares + r * r
                residual.append(r)
            for a in range(3):
                fix = jac[a, 0, x] * residual[0] + jac[a, 1, x] * residual[1] + jac[a, 2, x] * residual[2]
                new = uc[a, x] - fix
                uc[a, x] = new
                uy[0, a, x : x + 1, :] = new[0:1]
                uy[1, a, x : x + 1, :] = new[7:8]
        sq[pl.ds(it, 1), :] = jnp.sum(squares, axis=0, keepdims=True)

        @pl.when(it < ITERS - 1)
        def _():
            start_all(displacement_message, it + 1, 2 * it + 2)

        return carry

    sq[...] = jnp.zeros((8, 128), F32)
    lax.fori_loop(0, ITERS, iteration, 0)
    uout[...] = uc[...]

    def gather_sum(value, own, table, count, target_of, ssem, rsem):
        table[own] = value

        def copy(o):
            return pltpu.make_async_remote_copy(
                src_ref=sq,
                dst_ref=table.at[own],
                send_sem=ssem.at[o],
                recv_sem=rsem.at[o],
                device_id=target_of(o),
                device_id_type=MESH,
            )

        for o in range(1, count):
            copy(o).start()
        for o in range(1, count):
            copy(o).wait()
        total = table[0]
        for k in range(1, count):
            total = total + table[k]
        return total

    plane = gather_sum(
        sq[...],
        gy * 2 + gz,
        ara,
        2 * ny,
        lambda o: (gx, lax.rem(gy + o // 2, ny), lax.rem(gz + o, 2)),
        asend,
        arecv,
    )
    sq[...] = plane
    total = gather_sum(
        plane, gx, arb, nx, lambda o: (lax.rem(gx + o, nx), gy, gz), bsend, brecv
    )
    norms = jnp.sqrt(jnp.sum(total, axis=1, keepdims=True) / cells)
    for k in range(ITERS):
        nout[k] = jnp.sum(norms[k : k + 1, :])


def solution(mesh):
    nx, ny = mesh.shape["gx"], mesh.shape["gy"]

    def step(u_old, u_trial, jacobian_inverse, tile_base, pair_codes, pair_groups):
        tiles = tile_base.shape[0]
        cells = float(3 * 8 * 8 * 128 * nx * ny * mesh.shape["gz"])
        vmem = pl.BlockSpec(memory_space=pltpu.VMEM)
        smem = pl.BlockSpec(memory_space=pltpu.SMEM)
        v = pltpu.VMEM
        return pl.pallas_call(
            functools.partial(kernel, nx, ny, cells),
            out_shape=(
                jax.ShapeDtypeStruct(u_old.shape, F32),
                jax.ShapeDtypeStruct((ITERS,), F32),
            ),
            in_specs=[smem, vmem, vmem, vmem, vmem, vmem],
            out_specs=(vmem, smem),
            scratch_shapes=[
                v((3, 8, 8, 128), F32),
                v((2, 3, 8, 128), F32),
                v((ITERS, 3, 8, 8, 128), F32),
                v((ITERS, 2, 2, 3, 8, 128), F32),
                v((ITERS, 2, 2, 3, 8, 128), F32),
                v((ITERS, 2, 2, 2, 3, 8, 128), F32),
                v((3, 10, 8, 128), F32),
                v((3, 10, 8, 128), F32),
                v((2, 2, 3, 16, 128), F32),
                v((ITERS, 3, 8, 8, 128), F32),
                v((ITERS, 2, 2, 3, 8, 128), F32),
                v((ITERS, 2, 2, 3, 8, 128), F32),
                v((ITERS, 2, 2, 2, 3, 8, 128), F32),
                v((12, 64, 384), BF16),
                v((8, tiles, 384), F32),
                v((4, tiles, 128), I32),
                v((4, tiles, 128), I32),
                v((9, tiles, 128), F32),
                v((3, tiles, 128), F32),
                v((6, tiles, 128), F32),
                v((tiles, 128, 512), BF16),
                v((tiles, 128), F32),
                v((tiles, 128), F32),
                v((3, tiles * 8, 128), F32),
                v((8, 64, 384), F32),
                v((8, 128), F32),
                v((2 * ny, 8, 128), F32),
                v((nx, 8, 128), F32),
                pltpu.SemaphoreType.DMA((2 * ITERS, 18)),
                pltpu.SemaphoreType.DMA((2 * ITERS, 18)),
                pltpu.SemaphoreType.DMA((2 * ny,)),
                pltpu.SemaphoreType.DMA((2 * ny,)),
                pltpu.SemaphoreType.DMA((nx,)),
                pltpu.SemaphoreType.DMA((nx,)),
            ],
            compiler_params=pltpu.CompilerParams(
                collective_id=0, has_side_effects=True, vmem_limit_bytes=60 * 2**20
            ),
            name="relax",
        )(tile_base, u_old, u_trial, jacobian_inverse, pair_codes, pair_groups)

    everywhere = ("gx", "gy", "gz")
    return jax.shard_map(
        step,
        mesh=mesh,
        in_specs=(
            P(None, "gx", "gy", "gz"),
            P(None, "gx", "gy", "gz"),
            P(None, None, "gx", "gy", "gz"),
            P(everywhere),
            P(None, everywhere, None),
            P(everywhere, None),
        ),
        out_specs=(P(None, "gx", "gy", "gz"), P()),
        check_vma=False,
    )
```

time: 1840 us -> 71.2 us (0.04)
  starting transfers between devices: 927 us -> 0 us
  local copies, waits for them, and re-layouts: 401 us -> 2.06 us
  other arithmetic: 363 us -> 0 us
  blocking collectives: 108 us -> 0 us
  Pallas kernels: 0 us -> 68.3 us
  waiting for transfers between devices: 28.7 us -> 0 us
    ppermute x36 -> x0, starting transfers between devices: 927 us -> none  [the longest x18 846 us: shifted(): return lax.ppermute(shard, axis, pairs)]
    gather x168 -> x0, local copies, waits for them, and re-layouts: 339 us -> none  [pair_terms(): points.append(lattice + flat_u[:, flat_fn(node_cell)])]
    scatter-add x27 -> x0, other arithmetic: 337 us -> none  [the longest x21 337 us: one_block(): summed.at[:, flat_index.reshape(-1)].add(values.reshape(channels, -1))]
    psum x4 -> x0, blocking collectives: 108 us -> none  [over_axes(): shard = lax.psum(shard, axis)]
    pallas_call x0 -> x1, Pallas kernels: none -> 68.3 us  [step(): pl.pallas_call(functools.partial(kernel, nx, ny, cells), out_shape=(jax.S...]
    ppermute x36 -> x0, waiting for transfers between devices: 28.7 us -> none  [the longest x9 18.9 us: padded_2(): lax.ppermute(lax.slice_in_dim(block, 0, width, axis=dim), axis, backward)]
    while x6 -> x0, local copies, waits for them, and re-layouts: 26.3 us -> none  [accumulate(): summed = lax.fori_loop(0, block_turns, one_block, initial)]
  transfers between devices with their start and end apart: 36 -> 0, of which waited for: 16 -> 0; matrix products, arithmetic and copies ran while one was open for 0% -> 0% of each run, Pallas kernels for 0% -> 0%
where the time goes in v1:
time: 71.2 us; the launch traced here: 71 us
  Pallas kernels  68.3 us (96%)
  local copies, waits for them, and re-layouts  2.06 us (3%)
    pallas_call x1, Pallas kernels, step(): pl.pallas_call(functools.partial(kernel, nx, ny, cells), out_shape=(jax.S...  68.3 us
    unnamed x4, local copies, waits for them, and re-layouts  2.06 us

profile of v1, /device:TPU:1, one launch (start us, length us, event | category | flops | bytes accessed | tf_op | source)
XLA Modules:
  0.0 71.0 jit_solution(16747612642527234495)
XLA Ops:
  0.6 68.3 %relax.1 = (f32[3,8,8,128]{3,2,1,0:T(8,128)}, f32[3]{0:T(128)}) custom-call(s32[64]{0:T(128)} %tb_ref.1, f32[3,8,8,128]{3,2,1,0:T(8,128)} %uold.1, f32[3,8,8,128]{3,2,1,0:T(8,128)} %utrial.1, f32[3,3,8,8,128]{4,3,2,1,0:T(8,128)} %jac.1, s32[4,64,128]{2,1,0:T(8,128)} %codes.1, s32[64,128]{1,0:T(8,128)} %groups.1), custom_call_target="tpu_custom_call" | custom-call | tf_op jit(solution)/shard_map/relax/pallas_call | solution.py:450
  68.9 0.0 copy-start
  69.0 1.5 %copy.10 = f32[3,8,8,128]{3,2,1,0:T(8,128)} copy(f32[3,8,8,128]{3,2,1,0:T(8,128)} %get-tuple-element.4) | data formatting | bytes 196608
  70.5 0.0 copy-done
  70.5 0.5 copy.11
Async XLA Ops:
  68.9 1.6 %copy-start = (f32[3]{0:T(128)S(1)}, f32[3]{0:T(128)}, u32[]{:S(2)}) copy-start(f32[3]{0:T(128)} %get-tuple-element.5) | copy-start | bytes 40

commit v2 on v1

--- a/solution.py
+++ b/solution.py
@@ -13,13 +13,16 @@
 BF16 = jnp.bfloat16
 I32 = jnp.int32
 
-DIRS = [
-    (dx, dy, z)
-    for dx in (-1, 0, 1)
-    for dy in (-1, 0, 1)
-    for z in (0, 1)
-    if (dx, dy, z) != (0, 0, 0)
-]
+DIRS = sorted(
+    [
+        (dx, dy, z)
+        for dx in (-1, 0, 1)
+        for dy in (-1, 0, 1)
+        for z in (0, 1)
+        if (dx, dy, z) != (0, 0, 0)
+    ],
+    key=lambda d: (-2 * abs(d[0]) - abs(d[1]), d),
+)
 
 
 def slot_of(dx, dy, z):
@@ -39,15 +42,45 @@
     return hi, x - hi
 
 
+class Gathered:
+    def __init__(self, source, table, own, targets, send, recv):
+        self.source, self.table, self.own, self.targets = source, table, own, targets
+        self.send, self.recv = send, recv
+
+    def copy(self, o, device):
+        return pltpu.make_async_remote_copy(
+            src_ref=self.source,
+            dst_ref=self.table.at[self.own],
+            send_sem=self.send.at[o],
+            recv_sem=self.recv.at[o],
+            device_id=device,
+            device_id_type=MESH,
+        )
+
+    def start(self):
+        for o, device in self.targets:
+            self.copy(o, device).start()
+        self.table[self.own] = self.source[...]
+
+    def finish(self):
+        for o, device in self.targets:
+            self.copy(o, device).wait()
+        total = self.table[0]
+        for k in range(1, self.table.shape[0]):
+            total = total + self.table[k]
+        return total
+
+
 def kernel(
     nx, ny, cells,
-    tb_ref, uold, utrial, jac, codes, groups,
+    tb_in, uold_in, utrial_in, jac_in, codes_in, groups_in,
     uout, nout,
-    uc, uy, rxz, rxx, rxy, rxd,
-    pb, pz, yr, frz, frx, fry, frd,
-    win, gat, kidx, lidx, geo, frozen, halves, onehot, ohg, ohs, outs, acc,
-    sq, ara, arb,
-    send_sem, recv_sem, asend, arecv, bsend, brecv,
+    tb_ref, uold, jac, codes, groups, residuals,
+    uc, uy, uxe, uye, ud, rxz, rxx, rxy, rxxe, rxye, rxd,
+    pb, pz, yr, fxe, fye, fd, frz, frx, fry, frxe, frye, frd,
+    win, gat, kidx, lidx, geo, frozen, onehot, ohg, ohs, outs, acc,
+    sq, sq2, ara, arb,
+    in_sem, send_sem, recv_sem, asend, arecv, bsend, brecv,
 ):
     gx, gy, gz = lax.axis_index("gx"), lax.axis_index("gy"), lax.axis_index("gz")
     tiles = groups.shape[0]
@@ -87,28 +120,54 @@
     for o in range(1, nx):
         greet((lax.rem(gx + o, nx), gy, gz))
 
+    fetches = [
+        pltpu.make_async_copy(src, dst, in_sem.at[k])
+        for k, (src, dst) in enumerate(
+            [
+                (utrial_in, uc),
+                (tb_in, tb_ref),
+                (codes_in, codes),
+                (groups_in, groups),
+                (uold_in, uold),
+                (jac_in, jac),
+            ]
+        )
+    ]
+    for fetch in fetches:
+        fetch.start()
+
     def lo_hi(d):
         return 1 if d > 0 else 0
 
     def displacement_message(it, d):
         dx, dy, z = d
+        xi, yi = lo_hi(dx), lo_hi(dy)
         if dx == 0 and dy == 0:
             return uc, rxz.at[it]
         if dy == 0:
-            return uc.at[:, 7 * lo_hi(dx)], rxx.at[it, 1 - lo_hi(dx), z]
+            if z:
+                return uxe.at[xi], rxxe.at[it, 1 - xi]
+            return uc.at[:, 7 * xi], rxx.at[it, 1 - xi]
         if dx == 0:
-            return uy.at[lo_hi(dy)], rxy.at[it, 1 - lo_hi(dy), z]
-        return uy.at[lo_hi(dy)], rxd.at[it, 1 - lo_hi(dx), 1 - lo_hi(dy), z]
+            if z:
+                return uye.at[yi], rxye.at[it, 1 - yi]
+            return uy.at[yi], rxy.at[it, 1 - yi]
+        return ud.at[xi, yi], rxd.at[it, 1 - xi, 1 - yi, z]
 
     def force_message(it, d):
         dx, dy, z = d
+        xi, yi = lo_hi(dx), lo_hi(dy)
         if dx == 0 and dy == 0:
             return pz.at[:, 1:9], frz.at[it]
         if dy == 0:
-            return (pz if z else pb).at[:, 9 * lo_hi(dx)], frx.at[it, 1 - lo_hi(dx), z]
+            if z:
+                return fxe.at[xi], frxe.at[it, 1 - xi]
+            return pb.at[:, 9 * xi], frx.at[it, 1 - xi]
         if dx == 0:
-            return yr.at[z, lo_hi(dy), :, 0:8], fry.at[it, 1 - lo_hi(dy), z]
-        return yr.at[z, lo_hi(dy), :, 8:16], frd.at[it, 1 - lo_hi(dx), 1 - lo_hi(dy), z]
+            if z:
+                return fye.at[yi], frye.at[it, 1 - yi]
+            return yr.at[0, yi], fry.at[it, 1 - yi]
+        return fd.at[z, xi, yi], frd.at[it, 1 - xi, 1 - yi, z]
 
     def copy_of(message, it, phase, d):
         src, dst = message(it, d)
@@ -136,13 +195,41 @@
     row8 = iota((8, 128), 0)
     lane8 = iota((8, 128), 1)
 
-    def store_row_packs(read):
-        for c in range(3):
-            for x in range(8):
-                plane = read(c, x)
-                uy[0, c, x : x + 1, :] = plane[0:1]
-                uy[1, c, x : x + 1, :] = plane[7:8]
-
+    my_edge = jnp.where(gz == 0, 127, 0)
+    other_edge = 127 - my_edge
+    my_edge_index = jnp.full((8, 128), my_edge, I32)
+    other_edge_index = jnp.full((8, 128), other_edge, I32)
+    lane_index = [jnp.full((8, 128), c, I32) for c in range(3)]
+
+    def edges(planes, index):
+        packed = take(planes[0], index)
+        for c in (1, 2):
+            packed = jnp.where(lane8 == c, take(planes[c], index), packed)
+        return packed
+
+    def store_row_packs():
+        for xi, x in ((0, 0), (1, 7)):
+            uxe[xi] = edges([uc[c, x] for c in range(3)], my_edge_index)
+            for yi in range(2):
+                for c in range(3):
+                    ud[xi, yi, c : c + 1, :] = uy[yi, c, x : x + 1, :]
+        for yi in range(2):
+            uye[yi] = edges([uy[yi, c] for c in range(3)], my_edge_index)
+
+    fetches[0].wait()
+    for c in range(3):
+        for x in range(8):
+            plane = uc[c, x]
+            uy[0, c, x : x + 1, :] = plane[0:1]
+            uy[1, c, x : x + 1, :] = plane[7:8]
+    store_row_packs()
+    beside_x = (gx > 0).astype(I32) + (gx < nx - 1).astype(I32)
+    beside_y = (gy > 0).astype(I32) + (gy < ny - 1).astype(I32)
+    pl.semaphore_wait(barrier, 2 * (1 + beside_x) * (1 + beside_y) - 1 + 2 * ny - 1 + nx - 1)
+    start_all(displacement_message, 0, 0)
+
+    for fetch in fetches[1:]:
+        fetch.wait()
     lane_k = iota((8, 128), 1)
     for g in range(tiles // 8):
         base = jnp.zeros((8, 128), I32)
@@ -193,23 +280,18 @@
     win[0] = zero_plane
     win[11] = zero_plane
 
-    beside_x = (gx > 0).astype(I32) + (gx < nx - 1).astype(I32)
-    beside_y = (gy > 0).astype(I32) + (gy < ny - 1).astype(I32)
-    pl.semaphore_wait(barrier, 2 * (1 + beside_x) * (1 + beside_y) - 1 + 2 * ny - 1 + nx - 1)
-    uc[...] = utrial[...]
-    store_row_packs(lambda c, x: utrial[c, x])
-    start_all(displacement_message, 0, 0)
-
     row128 = iota((128, 128), 0)
 
     def make_onehot(t, carry):
-        for n in range(4):
-            row = lidx[n, pl.ds(t, 1), :]
-            sign = -1.0 if n < 2 else 1.0
-            onehot[t, :, n * 128 : (n + 1) * 128] = jnp.where(row128 == row, sign, 0.0).astype(BF16)
+        for n in range(2):
+            first = lidx[2 * n, pl.ds(t, 1), :]
+            second = lidx[2 * n + 1, pl.ds(t, 1), :]
+            sign = 1.0 if n else -1.0
+            flat = jnp.where(jnp.logical_or(row128 == first, row128 == second), sign, 0.0).astype(BF16)
+            onehot[t, n * 128 : (n + 1) * 128, :] = jnp.transpose(flat)
         return carry
 
-    lax.fori_loop(0, tiles, make_onehot, 0)
+    lax.fori_loop(0, tiles, make_onehot, 0, unroll=4)
     pick = ohg[...].astype(BF16)
     spread_t = jnp.transpose(ohs[...])[0:64, 0:tiles].astype(BF16)
     spread = jnp.concatenate([spread_t, spread_t], axis=1)
@@ -219,27 +301,45 @@
     edge_row = {0: row8 == 7, 1: row8 == 0}
     edge_lane = {0: lane8 == 127, 1: lane8 == 0}
     z_ok = {0: gz == 1, 1: gz == 0}
-    my_edge_lane = lane8 == jnp.where(gz == 0, 0, 127)
+    my_edge_lane = lane8 == other_edge
+    at_edge = lane8 == my_edge
+
+    first_sum = Gathered(
+        sq,
+        ara,
+        gy * 2 + gz,
+        [(o, (gx, lax.rem(gy + o // 2, ny), lax.rem(gz + o, 2))) for o in range(1, 2 * ny)],
+        asend,
+        arecv,
+    )
+    second_sum = Gathered(
+        sq2, arb, gx, [(o, (lax.rem(gx + o, nx), gy, gz)) for o in range(1, nx)], bsend, brecv
+    )
 
     def iteration(it, carry):
         wait_all(displacement_message, it, 2 * it)
 
+        beyond_rows = [
+            [take(valid(y_ok[dy], rxye[it, lo_hi(dy)]), lane_index[c]) for c in range(3)] for dy in (-1, 1)
+        ]
         for x in range(10):
             for c in range(3):
                 if 1 <= x <= 8:
                     own, other = uc[c, x - 1], rxz[it, c, x - 1]
                     rows = [
-                        [valid(y_ok[dy], rxy[it, lo_hi(dy), z, c, x - 1 : x, :]) for z in (0, 1)]
+                        [
+                            valid(y_ok[dy], rxy[it, lo_hi(dy), c, x - 1 : x, :]),
+                            beyond_rows[lo_hi(dy)][c][x - 1 : x],
+                        ]
                         for dy in (-1, 1)
                     ]
                 else:
                     dx, xi = (-1, 0) if x == 0 else (1, 1)
-                    own = valid(x_ok[dx], rxx[it, xi, 0, c])
-                    other = valid(x_ok[dx], rxx[it, xi, 1, c])
-                    at = 7 if x == 0 else 0
+                    own = valid(x_ok[dx], rxx[it, xi, c])
+                    other = take(valid(x_ok[dx], rxxe[it, xi]), lane_index[c])
                     rows = [
                         [
-                            valid(exists(dx, dy), rxd[it, xi, lo_hi(dy), z, c, at : at + 1, :])
+                            valid(exists(dx, dy), rxd[it, xi, lo_hi(dy), z, c : c + 1, :])
                             for z in (0, 1)
                         ]
                         for dy in (-1, 1)
@@ -264,7 +364,7 @@
 
         live_below = jnp.where(it == 0, 2, 1)
 
-        def group(g, carry):
+        def pair_forces(g):
             at = pl.ds(pl.multiple_of(g * 8, 8), 8)
             points = []
             for n in range(4):
@@ -289,32 +389,40 @@
             dots = one[0] * two[0] + one[1] * two[1] + one[2] * two[2]
             coupling = 0.5 * dots / (square * jnp.sqrt(square))
             fresh = groups[at, :] < live_below
+            values = []
             for c in range(3):
                 force = jnp.where(fresh, coupling * apart[c], frozen[c, at, :])
                 frozen[c, at, :] = force
-                hi, lo = split(0.5 * force)
-                halves[2 * c, at, :] = hi
-                halves[2 * c + 1, at, :] = lo
+                values.extend(split(0.5 * force))
+            return tuple(values)
+
+        def spread_forces(g, values):
             for i in range(8):
                 t = g * 8 + i
-                values = [halves[q, pl.ds(t, 1), :] for q in range(6)]
                 columns = []
-                for n in range(4):
-                    mask = row8 == kidx[n, pl.ds(t, 1), :]
+                for n in range(2):
+                    mask = jnp.logical_or(
+                        row8 == kidx[2 * n, pl.ds(t, 1), :], row8 == kidx[2 * n + 1, pl.ds(t, 1), :]
+                    )
                     columns.append(
-                        jnp.concatenate([jnp.where(mask, v, 0.0) for v in values], axis=0).astype(BF16)
+                        jnp.concatenate(
+                            [jnp.where(mask, v[i : i + 1], 0.0) for v in values], axis=0
+                        ).astype(BF16)
                     )
                 lhs = jnp.concatenate(columns, axis=1)
-                got = lax.dot_general(
-                    lhs, onehot[t], (((1,), (1,)), ((), ())), preferred_element_type=F32
-                )
+                got = jnp.dot(lhs, onehot[t], preferred_element_type=F32)
                 for c in range(3):
                     outs[c, pl.ds(pl.multiple_of(t * 8, 8), 8), :] = (
                         got[16 * c : 16 * c + 8] + got[16 * c + 8 : 16 * c + 16]
                     )
-            return carry
-
-        lax.fori_loop(0, tiles // 8, group, 0)
+
+        def group(g, values):
+            later = pair_forces(g)
+            spread_forces(g - 1, values)
+            return later
+
+        values = lax.fori_loop(1, tiles // 8, group, pair_forces(0))
+        spread_forces(tiles // 8 - 1, values)
 
         for k in range(8):
             columns = []
@@ -345,97 +453,93 @@
                         line = inside if line is None else line + inside
                         beyond = outside if beyond is None else beyond + outside
                     parts.append((line, jnp.where(my_edge_lane, beyond, 0.0)))
-                row_at = (x + 15) % 16
                 for z in range(2):
                     (pz if z else pb)[c, x] = jnp.where(edge_row[0], 0.0, parts[0][z]) + jnp.where(
                         edge_row[1], 0.0, parts[1][z]
                     )
-                    yr[z, 0, c, row_at : row_at + 1, :] = parts[0][z][7:8]
-                    yr[z, 1, c, row_at : row_at + 1, :] = parts[1][z][0:1]
+                    ends = (parts[0][z][7:8], parts[1][z][0:1])
+                    for yi in range(2):
+                        if 1 <= x <= 8:
+                            yr[z, yi, c, x - 1 : x, :] = ends[yi]
+                        else:
+                            fd[z, 0 if x == 0 else 1, yi, c : c + 1, :] = ends[yi]
+        for i in range(2):
+            fxe[i] = edges([pz[c, 9 * i] for c in range(3)], other_edge_index)
+            fye[i] = edges([yr[1, i, c] for c in range(3)], other_edge_index)
         start_all(force_message, it, 2 * it + 1)
         wait_all(force_message, it, 2 * it + 1)
 
         squares = jnp.zeros((8, 128), F32)
+        lines = []
+        for dy in (-1, 1):
+            yi = lo_hi(dy)
+            lines.append(
+                [
+                    valid(
+                        y_ok[dy],
+                        fry[it, yi, c] + jnp.where(at_edge, take(frye[it, yi], lane_index[c]), 0.0),
+                    )
+                    for c in range(3)
+                ]
+            )
         for x in range(8):
-            residual = []
             for c in range(3):
                 total = pb[c, x + 1] + frz[it, c, x]
                 for dx, xe in ((-1, 0), (1, 7)):
                     if x == xe:
                         xi = lo_hi(dx)
-                        total = total + valid(x_ok[dx], frx[it, xi, 0, c] + frx[it, xi, 1, c])
+                        total = total + valid(
+                            x_ok[dx],
+                            frx[it, xi, c] + jnp.where(at_edge, take(frxe[it, xi], lane_index[c]), 0.0),
+                        )
                 for dy in (-1, 1):
                     yi = lo_hi(dy)
-                    line = valid(
-                        y_ok[dy], fry[it, yi, 0, c, x : x + 1, :] + fry[it, yi, 1, c, x : x + 1, :]
-                    )
-                    for dx, xe, rd in ((-1, 0, 0), (1, 7, 7)):
+                    line = lines[yi][c][x : x + 1]
+                    for dx, xe in ((-1, 0), (1, 7)):
                         if x == xe:
                             xi = lo_hi(dx)
                             line = line + valid(
                                 exists(dx, dy),
-                                frd[it, xi, yi, 0, c, rd : rd + 1, :] + frd[it, xi, yi, 1, c, rd : rd + 1, :],
+                                frd[it, xi, yi, 0, c : c + 1, :] + frd[it, xi, yi, 1, c : c + 1, :],
                             )
                     total = total + jnp.where(row8 == (0 if dy < 0 else 7), line, 0.0)
                 r = uc[c, x] - uold[c, x] - 0.5 * total
                 squares = squares + r * r
-                residual.append(r)
+                residuals[c, x] = r
+        sq[pl.ds(it, 1), :] = jnp.sum(squares, axis=0, keepdims=True)
+
+        @pl.when(it == ITERS - 1)
+        def _():
+            first_sum.start()
+
+        for x in range(8):
+            residual = [residuals[c, x] for c in range(3)]
             for a in range(3):
                 fix = jac[a, 0, x] * residual[0] + jac[a, 1, x] * residual[1] + jac[a, 2, x] * residual[2]
                 new = uc[a, x] - fix
                 uc[a, x] = new
                 uy[0, a, x : x + 1, :] = new[0:1]
                 uy[1, a, x : x + 1, :] = new[7:8]
-        sq[pl.ds(it, 1), :] = jnp.sum(squares, axis=0, keepdims=True)
 
         @pl.when(it < ITERS - 1)
         def _():
+            store_row_packs()
             start_all(displacement_message, it + 1, 2 * it + 2)
 
         return carry
 
     sq[...] = jnp.zeros((8, 128), F32)
     lax.fori_loop(0, ITERS, iteration, 0)
-    uout[...] = uc[...]
-
-    def gather_sum(value, own, table, count, target_of, ssem, rsem):
-        table[own] = value
-
-        def copy(o):
-            return pltpu.make_async_remote_copy(
-                src_ref=sq,
-                dst_ref=table.at[own],
-                send_sem=ssem.at[o],
-                recv_sem=rsem.at[o],
-                device_id=target_of(o),
-                device_id_type=MESH,
-            )
-
-        for o in range(1, count):
-            copy(o).start()
-        for o in range(1, count):
-            copy(o).wait()
-        total = table[0]
-        for k in range(1, count):
-            total = total + table[k]
-        return total
-
-    plane = gather_sum(
-        sq[...],
-        gy * 2 + gz,
-        ara,
-        2 * ny,
-        lambda o: (gx, lax.rem(gy + o // 2, ny), lax.rem(gz + o, 2)),
-        asend,
-        arecv,
-    )
-    sq[...] = plane
-    total = gather_sum(
-        plane, gx, arb, nx, lambda o: (lax.rem(gx + o, nx), gy, gz), bsend, brecv
-    )
+    store_result = pltpu.make_async_copy(uc, uout, in_sem.at[0])
+    store_result.start()
+    plane = first_sum.finish()
+    second_sum.source[...] = plane
+    second_sum.start()
+    total = second_sum.finish()
     norms = jnp.sqrt(jnp.sum(total, axis=1, keepdims=True) / cells)
     for k in range(ITERS):
         nout[k] = jnp.sum(norms[k : k + 1, :])
+    store_result.wait()
 
 
 def solution(mesh):
@@ -444,7 +548,6 @@
     def step(u_old, u_trial, jacobian_inverse, tile_base, pair_codes, pair_groups):
         tiles = tile_base.shape[0]
         cells = float(3 * 8 * 8 * 128 * nx * ny * mesh.shape["gz"])
-        vmem = pl.BlockSpec(memory_space=pltpu.VMEM)
         smem = pl.BlockSpec(memory_space=pltpu.SMEM)
         v = pltpu.VMEM
         return pl.pallas_call(
@@ -453,37 +556,54 @@
                 jax.ShapeDtypeStruct(u_old.shape, F32),
                 jax.ShapeDtypeStruct((ITERS,), F32),
             ),
-            in_specs=[smem, vmem, vmem, vmem, vmem, vmem],
-            out_specs=(vmem, smem),
+            in_specs=[pl.BlockSpec(memory_space=pl.ANY)] * 6,
+            out_specs=(pl.BlockSpec(memory_space=pl.ANY), smem),
             scratch_shapes=[
+                pltpu.SMEM(tile_base.shape, I32),
+                v(u_old.shape, F32),
+                v(jacobian_inverse.shape, F32),
+                v(pair_codes.shape, I32),
+                v(pair_groups.shape, I32),
+                v(u_old.shape, F32),
                 v((3, 8, 8, 128), F32),
                 v((2, 3, 8, 128), F32),
+                v((2, 8, 128), F32),
+                v((2, 8, 128), F32),
+                v((2, 2, 8, 128), F32),
                 v((ITERS, 3, 8, 8, 128), F32),
-                v((ITERS, 2, 2, 3, 8, 128), F32),
-                v((ITERS, 2, 2, 3, 8, 128), F32),
-                v((ITERS, 2, 2, 2, 3, 8, 128), F32),
+                v((ITERS, 2, 3, 8, 128), F32),
+                v((ITERS, 2, 3, 8, 128), F32),
+                v((ITERS, 2, 8, 128), F32),
+                v((ITERS, 2, 8, 128), F32),
+                v((ITERS, 2, 2, 2, 8, 128), F32),
                 v((3, 10, 8, 128), F32),
                 v((3, 10, 8, 128), F32),
-                v((2, 2, 3, 16, 128), F32),
+                v((2, 2, 3, 8, 128), F32),
+                v((2, 8, 128), F32),
+                v((2, 8, 128), F32),
+                v((2, 2, 2, 8, 128), F32),
                 v((ITERS, 3, 8, 8, 128), F32),
-                v((ITERS, 2, 2, 3, 8, 128), F32),
-                v((ITERS, 2, 2, 3, 8, 128), F32),
-                v((ITERS, 2, 2, 2, 3, 8, 128), F32),
+                v((ITERS, 2, 3, 8, 128), F32),
+                v((ITERS, 2, 3, 8, 128), F32),
+                v((ITERS, 2, 8, 128), F32),
+                v((ITERS, 2, 8, 128), F32),
+                v((ITERS, 2, 2, 2, 8, 128), F32),
                 v((12, 64, 384), BF16),
                 v((8, tiles, 384), F32),
                 v((4, tiles, 128), I32),
                 v((4, tiles, 128), I32),
                 v((9, tiles, 128), F32),
                 v((3, tiles, 128), F32),
-                v((6, tiles, 128), F32),
-                v((tiles, 128, 512), BF16),
+                v((tiles, 256, 128), BF16),
                 v((tiles, 128), F32),
                 v((tiles, 128), F32),
                 v((3, tiles * 8, 128), F32),
                 v((8, 64, 384), F32),
                 v((8, 128), F32),
+                v((8, 128), F32),
                 v((2 * ny, 8, 128), F32),
                 v((nx, 8, 128), F32),
+                pltpu.SemaphoreType.DMA((6,)),
                 pltpu.SemaphoreType.DMA((2 * ITERS, 18)),
                 pltpu.SemaphoreType.DMA((2 * ITERS, 18)),
                 pltpu.SemaphoreType.DMA((2 * ny,)),

time: 71.2 us -> 57.2 us (0.80)
  Pallas kernels: 68.3 us -> 54.4 us
    pallas_call x1, Pallas kernels: 68.3 us -> 54.4 us  [step(): pl.pallas_call(functools.partial(kernel, nx, ny, cells), out_shape=(jax.S...]
where the time goes in v2:
time: 57.2 us; the launch traced here: 57.1 us
  Pallas kernels  54.4 us (95%)
  local copies, waits for them, and re-layouts  2.06 us (4%)
  between operations  0.65 us (1%)
    pallas_call x1, Pallas kernels, step(): pl.pallas_call(functools.partial(kernel, nx, ny, cells), out_shape=(jax.S...  54.4 us
    unnamed x4, local copies, waits for them, and re-layouts  2.06 us

profile of v2, /device:TPU:1, one launch (start us, length us, event | category | flops | bytes accessed | tf_op | source)
XLA Modules:
  0.0 57.1 jit_solution(2115406305820093540)
XLA Ops:
  0.6 54.4 %relax.1 = (f32[3,8,8,128]{3,2,1,0:T(8,128)}, f32[3]{0:T(128)}) custom-call(s32[64]{0:T(128)} %tb_in.1, f32[3,8,8,128]{3,2,1,0:T(8,128)} %uold_in.1, f32[3,8,8,128]{3,2,1,0:T(8,128)} %utrial_in.1, f32[3,3,8,8,128]{4,3,2,1,0:T(8,128)} %jac_in.1, s32[4,64,128]{2,1,0:T(8,128)} %codes_in.1, s32[64,128]{1,0:T(8,128)} %groups_in.1), custom_call_target="tpu_custom_call" | custom-call | tf_op jit(solution)/shard_map/relax/pallas_call | solution.py:553
  55.0 0.0 copy-start
  55.0 1.5 %copy.10 = f32[3,8,8,128]{3,2,1,0:T(8,128)} copy(f32[3,8,8,128]{3,2,1,0:T(8,128)} %get-tuple-element.4) | data formatting | bytes 196608
  56.6 0.0 copy-done
  56.6 0.5 copy.11
Async XLA Ops:
  55.0 1.6 %copy-start = (f32[3]{0:T(128)S(1)}, f32[3]{0:T(128)}, u32[]{:S(2)}) copy-start(f32[3]{0:T(128)} %get-tuple-element.5) | copy-start | bytes 40

commit v3 on v2

--- a/solution.py
+++ b/solution.py
@@ -25,6 +25,10 @@
 )
 
 
+FAR = [d for d in DIRS if d[0] != 0]
+NEAR = [d for d in DIRS if d[0] == 0]
+
+
 def slot_of(dx, dy, z):
     return ((dx + 1) * 3 + dy + 1) * 2 + z
 
@@ -80,7 +84,7 @@
     pb, pz, yr, fxe, fye, fd, frz, frx, fry, frxe, frye, frd,
     win, gat, kidx, lidx, geo, frozen, onehot, ohg, ohs, outs, acc,
     sq, sq2, ara, arb,
-    in_sem, send_sem, recv_sem, asend, arecv, bsend, brecv,
+    hail_four, hail_eight, in_sem, send_sem, recv_sem, asend, arecv, bsend, brecv,
 ):
     gx, gy, gz = lax.axis_index("gx"), lax.axis_index("gy"), lax.axis_index("gz")
     tiles = groups.shape[0]
@@ -115,10 +119,6 @@
 
     for d in DIRS:
         guarded(exists(d[0], d[1]), functools.partial(greet, target(*d)))
-    for o in range(1, 2 * ny):
-        greet((gx, lax.rem(gy + o // 2, ny), lax.rem(gz + o, 2)))
-    for o in range(1, nx):
-        greet((lax.rem(gx + o, nx), gy, gz))
 
     fetches = [
         pltpu.make_async_copy(src, dst, in_sem.at[k])
@@ -181,14 +181,16 @@
             device_id_type=MESH,
         )
 
-    def start_all(message, it, phase):
-        for d in DIRS:
+    def start(message, it, phase, dirs):
+        for d in dirs:
             guarded(exists(d[0], d[1]), lambda d=d: copy_of(message, it, phase, d).start())
 
-    def wait_all(message, it, phase):
-        for d in DIRS:
+    def wait_arrivals(message, it, phase, dirs):
+        for d in dirs:
             back = (-d[0], -d[1], d[2])
             guarded(exists(d[0], d[1]), lambda d=back: copy_of(message, it, phase, d).wait_recv())
+
+    def wait_sends(message, it, phase):
         for d in DIRS:
             guarded(exists(d[0], d[1]), lambda d=d: copy_of(message, it, phase, d).wait_send())
 
@@ -207,12 +209,14 @@
             packed = jnp.where(lane8 == c, take(planes[c], index), packed)
         return packed
 
-    def store_row_packs():
+    def pack_far():
         for xi, x in ((0, 0), (1, 7)):
             uxe[xi] = edges([uc[c, x] for c in range(3)], my_edge_index)
             for yi in range(2):
                 for c in range(3):
                     ud[xi, yi, c : c + 1, :] = uy[yi, c, x : x + 1, :]
+
+    def pack_near():
         for yi in range(2):
             uye[yi] = edges([uy[yi, c] for c in range(3)], my_edge_index)
 
@@ -222,11 +226,12 @@
             plane = uc[c, x]
             uy[0, c, x : x + 1, :] = plane[0:1]
             uy[1, c, x : x + 1, :] = plane[7:8]
-    store_row_packs()
+    pack_far()
+    pack_near()
     beside_x = (gx > 0).astype(I32) + (gx < nx - 1).astype(I32)
     beside_y = (gy > 0).astype(I32) + (gy < ny - 1).astype(I32)
-    pl.semaphore_wait(barrier, 2 * (1 + beside_x) * (1 + beside_y) - 1 + 2 * ny - 1 + nx - 1)
-    start_all(displacement_message, 0, 0)
+    pl.semaphore_wait(barrier, 2 * (1 + beside_x) * (1 + beside_y) - 1)
+    start(displacement_message, 0, 0, DIRS)
 
     for fetch in fetches[1:]:
         fetch.wait()
@@ -316,13 +321,27 @@
         sq2, arb, gx, [(o, (lax.rem(gx + o, nx), gy, gz)) for o in range(1, nx)], bsend, brecv
     )
 
+    def hail(semaphore, width):
+        for dx in (-width, width):
+            cond = gx + dx >= 0 if dx < 0 else gx + dx < nx
+
+            def signal(dx=dx):
+                pl.semaphore_signal(
+                    semaphore, inc=1, device_id=(gx + dx, gy, gz), device_id_type=MESH
+                )
+
+            pl.when(cond)(signal)
+
+    def hear(semaphore, width):
+        pl.semaphore_wait(semaphore, (gx >= width).astype(I32) + (gx + width < nx).astype(I32))
+
     def iteration(it, carry):
-        wait_all(displacement_message, it, 2 * it)
+        wait_arrivals(displacement_message, it, 2 * it, NEAR)
 
         beyond_rows = [
             [take(valid(y_ok[dy], rxye[it, lo_hi(dy)]), lane_index[c]) for c in range(3)] for dy in (-1, 1)
         ]
-        for x in range(10):
+        def make_windows(x):
             for c in range(3):
                 if 1 <= x <= 8:
                     own, other = uc[c, x - 1], rxz[it, c, x - 1]
@@ -358,9 +377,27 @@
                     hi, lo = split(both)
                     win[x + 1, s * 16 : s * 16 + 16, c * 128 : (c + 1) * 128] = hi.astype(BF16)
                     win[x + 1, 32 + s * 16 : 48 + s * 16, c * 128 : (c + 1) * 128] = lo.astype(BF16)
-        for k in range(8):
+
+        def hand_out(k):
             both = jnp.concatenate([win[k], win[k + 4]], axis=0)
             gat[k] = jnp.dot(pick, both, preferred_element_type=F32)
+
+        for x in range(1, 9):
+            make_windows(x)
+        for k in (0, 2, 3, 4, 5, 7):
+            hand_out(k)
+        wait_arrivals(displacement_message, it, 2 * it, FAR)
+        for x in (0, 9):
+            make_windows(x)
+        for k in (1, 6):
+            hand_out(k)
+
+        @pl.when(it == 2)
+        def _():
+            hear(hail_four, 4)
+            hail(hail_eight, 8)
+
+        wait_sends(displacement_message, it, 2 * it)
 
         live_below = jnp.where(it == 0, 2, 1)
 
@@ -424,14 +461,14 @@
         values = lax.fori_loop(1, tiles // 8, group, pair_forces(0))
         spread_forces(tiles // 8 - 1, values)
 
-        for k in range(8):
+        def collect(k):
             columns = []
             for c in range(3):
                 hi, lo = split(outs[c, pl.ds(k, tiles, stride=8), :])
                 columns.append(jnp.concatenate([hi, lo], axis=0).astype(BF16))
             acc[k] = jnp.dot(spread, jnp.concatenate(columns, axis=1), preferred_element_type=F32)
 
-        for x in range(10):
+        def fold(x):
             for c in range(3):
                 cut = slice(c * 128, (c + 1) * 128)
                 parts = []
@@ -463,13 +500,23 @@
                             yr[z, yi, c, x - 1 : x, :] = ends[yi]
                         else:
                             fd[z, 0 if x == 0 else 1, yi, c : c + 1, :] = ends[yi]
+
+        for k in (1, 6):
+            collect(k)
+        for x in (0, 9):
+            fold(x)
         for i in range(2):
             fxe[i] = edges([pz[c, 9 * i] for c in range(3)], other_edge_index)
+        start(force_message, it, 2 * it + 1, FAR)
+        for k in (0, 2, 3, 4, 5, 7):
+            collect(k)
+        for x in range(1, 9):
+            fold(x)
+        for i in range(2):
             fye[i] = edges([yr[1, i, c] for c in range(3)], other_edge_index)
-        start_all(force_message, it, 2 * it + 1)
-        wait_all(force_message, it, 2 * it + 1)
-
-        squares = jnp.zeros((8, 128), F32)
+        start(force_message, it, 2 * it + 1, NEAR)
+        wait_arrivals(force_message, it, 2 * it + 1, NEAR)
+
         lines = []
         for dy in (-1, 1):
             yi = lo_hi(dy)
@@ -482,7 +529,7 @@
                     for c in range(3)
                 ]
             )
-        for x in range(8):
+        def residual_of(x, squares):
             for c in range(3):
                 total = pb[c, x + 1] + frz[it, c, x]
                 for dx, xe in ((-1, 0), (1, 7)):
@@ -506,13 +553,9 @@
                 r = uc[c, x] - uold[c, x] - 0.5 * total
                 squares = squares + r * r
                 residuals[c, x] = r
-        sq[pl.ds(it, 1), :] = jnp.sum(squares, axis=0, keepdims=True)
-
-        @pl.when(it == ITERS - 1)
-        def _():
-            first_sum.start()
-
-        for x in range(8):
+            return squares
+
+        def update(x):
             residual = [residuals[c, x] for c in range(3)]
             for a in range(3):
                 fix = jac[a, 0, x] * residual[0] + jac[a, 1, x] * residual[1] + jac[a, 2, x] * residual[2]
@@ -521,10 +564,39 @@
                 uy[0, a, x : x + 1, :] = new[0:1]
                 uy[1, a, x : x + 1, :] = new[7:8]
 
+        squares = jnp.zeros((8, 128), F32)
+        for x in range(1, 7):
+            squares = residual_of(x, squares)
+        for x in range(1, 7):
+            update(x)
+        wait_arrivals(force_message, it, 2 * it + 1, FAR)
+
+        @pl.when(it == 1)
+        def _():
+            hail(hail_four, 4)
+
+        @pl.when(it == 2)
+        def _():
+            hear(hail_eight, 8)
+
+        for x in (0, 7):
+            squares = residual_of(x, squares)
+        sq[pl.ds(it, 1), :] = jnp.sum(squares, axis=0, keepdims=True)
+
+        @pl.when(it == ITERS - 1)
+        def _():
+            first_sum.start()
+
+        for x in (0, 7):
+            update(x)
+        wait_sends(force_message, it, 2 * it + 1)
+
         @pl.when(it < ITERS - 1)
         def _():
-            store_row_packs()
-            start_all(displacement_message, it + 1, 2 * it + 2)
+            pack_far()
+            start(displacement_message, it + 1, 2 * it + 2, FAR)
+            pack_near()
+            start(displacement_message, it + 1, 2 * it + 2, NEAR)
 
         return carry
 
@@ -556,7 +628,7 @@
                 jax.ShapeDtypeStruct(u_old.shape, F32),
                 jax.ShapeDtypeStruct((ITERS,), F32),
             ),
-            in_specs=[pl.BlockSpec(memory_space=pl.ANY)] * 6,
+            in_specs=[pl.BlockSpec(memory_space=pltpu.HBM)] * 6,
             out_specs=(pl.BlockSpec(memory_space=pl.ANY), smem),
             scratch_shapes=[
                 pltpu.SMEM(tile_base.shape, I32),
@@ -603,6 +675,8 @@
                 v((8, 128), F32),
                 v((2 * ny, 8, 128), F32),
                 v((nx, 8, 128), F32),
+                pltpu.SemaphoreType.REGULAR,
+                pltpu.SemaphoreType.REGULAR,
                 pltpu.SemaphoreType.DMA((6,)),
                 pltpu.SemaphoreType.DMA((2 * ITERS, 18)),
                 pltpu.SemaphoreType.DMA((2 * ITERS, 18)),
@@ -612,10 +686,15 @@
                 pltpu.SemaphoreType.DMA((nx,)),
             ],
             compiler_params=pltpu.CompilerParams(
-                collective_id=0, has_side_effects=True, vmem_limit_bytes=60 * 2**20
+                collective_id=0, has_side_effects=True, vmem_limit_bytes=24 * 2**20
             ),
             name="relax",
-        )(tile_base, u_old, u_trial, jacobian_inverse, pair_codes, pair_groups)
+        )(
+            *(
+                pltpu.with_memory_space_constraint(a, pltpu.HBM)
+                for a in (tile_base, u_old, u_trial, jacobian_inverse, pair_codes, pair_groups)
+            )
+        )
 
     everywhere = ("gx", "gy", "gz")
     return jax.shard_map(

time: 57.2 us -> 54.8 us (0.958)
  Pallas kernels: 54.4 us -> 52.9 us
  local copies, waits for them, and re-layouts: 2.06 us -> 1.15 us
    pallas_call x1, Pallas kernels: 54.4 us -> 52.9 us  [step(): pl.pallas_call(functools.partial(kernel, nx, ny, cells), out_shape=(jax.S...]
    unnamed x4 -> x2, local copies, waits for them, and re-layouts: 2.06 us -> 1.15 us
where the time goes in v3:
time: 54.8 us; the launch traced here: 54.7 us
  Pallas kernels  52.9 us (97%)
  local copies, waits for them, and re-layouts  1.15 us (2%)
  between operations  0.64 us (1%)
    pallas_call x1, Pallas kernels, step(): pl.pallas_call(functools.partial(kernel, nx, ny, cells), out_shape=(jax.S...  52.9 us
    unnamed x2, local copies, waits for them, and re-layouts  1.15 us

profile of v3, /device:TPU:1, one launch (start us, length us, event | category | flops | bytes accessed | tf_op | source)
XLA Modules:
  0.0 54.7 jit_solution(17498784003510649071)
XLA Ops:
  0.6 52.9 %relax.1 = (f32[3,8,8,128]{3,2,1,0:T(8,128)S(1)}, f32[3]{0:T(128)S(1)}) custom-call(s32[64]{0:T(128)} %tb_in.1, f32[3,8,8,128]{3,2,1,0:T(8,128)} %uold_in.1, f32[3,8,8,128]{3,2,1,0:T(8,128)} %utrial_in.1, f32[3,3,8,8,128]{4,3,2,1,0:T(8,128)} %jac_in.1, s32[4,64,128]{2,1,0:T(8,128)} %codes_in.1, s32[64,128]{1,0:T(8,128)} %groups_in.1), custom_call_target="tpu_custom_call" | custom-call | tf_op jit(solution)/shard_map/relax/pallas_call | solution.py:625
  53.5 0.6 %copy.10 = f32[3,8,8,128]{3,2,1,0:T(8,128)} copy(f32[3,8,8,128]{3,2,1,0:T(8,128)S(1)} %get-tuple-element.4) | data formatting | bytes 196608
  54.2 0.5 copy.11

commit v4 on v3

--- a/solution.py
+++ b/solution.py
@@ -46,35 +46,6 @@
     return hi, x - hi
 
 
-class Gathered:
-    def __init__(self, source, table, own, targets, send, recv):
-        self.source, self.table, self.own, self.targets = source, table, own, targets
-        self.send, self.recv = send, recv
-
-    def copy(self, o, device):
-        return pltpu.make_async_remote_copy(
-            src_ref=self.source,
-            dst_ref=self.table.at[self.own],
-            send_sem=self.send.at[o],
-            recv_sem=self.recv.at[o],
-            device_id=device,
-            device_id_type=MESH,
-        )
-
-    def start(self):
-        for o, device in self.targets:
-            self.copy(o, device).start()
-        self.table[self.own] = self.source[...]
-
-    def finish(self):
-        for o, device in self.targets:
-            self.copy(o, device).wait()
-        total = self.table[0]
-        for k in range(1, self.table.shape[0]):
-            total = total + self.table[k]
-        return total
-
-
 def kernel(
     nx, ny, cells,
     tb_in, uold_in, utrial_in, jac_in, codes_in, groups_in,
@@ -83,8 +54,8 @@
     uc, uy, uxe, uye, ud, rxz, rxx, rxy, rxxe, rxye, rxd,
     pb, pz, yr, fxe, fye, fd, frz, frx, fry, frxe, frye, frd,
     win, gat, kidx, lidx, geo, frozen, onehot, ohg, ohs, outs, acc,
-    sq, sq2, ara, arb,
-    hail_four, hail_eight, in_sem, send_sem, recv_sem, asend, arecv, bsend, brecv,
+    sq, total_row, table,
+    hail_four, hail_eight, in_sem, send_sem, recv_sem, total_send, total_recv,
 ):
     gx, gy, gz = lax.axis_index("gx"), lax.axis_index("gy"), lax.axis_index("gz")
     tiles = groups.shape[0]
@@ -181,18 +152,24 @@
             device_id_type=MESH,
         )
 
+    def grouped(dirs, act):
+        for dx, dy in dict.fromkeys((d[0], d[1]) for d in dirs):
+
+            def both(dx=dx, dy=dy):
+                for d in dirs:
+                    if (d[0], d[1]) == (dx, dy):
+                        act(d)
+
+            guarded(exists(dx, dy), both)
+
     def start(message, it, phase, dirs):
-        for d in dirs:
-            guarded(exists(d[0], d[1]), lambda d=d: copy_of(message, it, phase, d).start())
+        grouped(dirs, lambda d: copy_of(message, it, phase, d).start())
 
     def wait_arrivals(message, it, phase, dirs):
-        for d in dirs:
-            back = (-d[0], -d[1], d[2])
-            guarded(exists(d[0], d[1]), lambda d=back: copy_of(message, it, phase, d).wait_recv())
+        grouped(dirs, lambda d: copy_of(message, it, phase, (-d[0], -d[1], d[2])).wait_recv())
 
     def wait_sends(message, it, phase):
-        for d in DIRS:
-            guarded(exists(d[0], d[1]), lambda d=d: copy_of(message, it, phase, d).wait_send())
+        grouped(DIRS, lambda d: copy_of(message, it, phase, d).wait_send())
 
     row8 = iota((8, 128), 0)
     lane8 = iota((8, 128), 1)
@@ -309,17 +286,30 @@
     my_edge_lane = lane8 == other_edge
     at_edge = lane8 == my_edge
 
-    first_sum = Gathered(
-        sq,
-        ara,
-        gy * 2 + gz,
-        [(o, (gx, lax.rem(gy + o // 2, ny), lax.rem(gz + o, 2))) for o in range(1, 2 * ny)],
-        asend,
-        arecv,
+    count = 2 * nx * ny
+    me = (gx * ny + gy) * 2 + gz
+
+    xs = [lax.rem(gx + a, nx) for a in range(nx)]
+    ys = [lax.rem(gy + b, ny) for b in range(ny)]
+
+    def ring(o, n):
+        return min(o, n - o)
+
+    offsets = [(a, b, c) for a in range(nx) for b in range(ny) for c in range(2) if (a, b, c) != (0, 0, 0)]
+    offsets.sort(
+        key=lambda o: -(ring(o[0] // 4, nx // 4) + ring(o[0] % 4, 4) + ring(o[1], ny))
     )
-    second_sum = Gathered(
-        sq2, arb, gx, [(o, (lax.rem(gx + o, nx), gy, gz)) for o in range(1, nx)], bsend, brecv
-    )
+
+    def send_squares():
+        for a, b, c in offsets:
+            pltpu.make_async_remote_copy(
+                src_ref=total_row,
+                dst_ref=table.at[me],
+                send_sem=total_send,
+                recv_sem=total_recv,
+                device_id=(xs[a], ys[b], 1 - gz if c else gz),
+                device_id_type=MESH,
+            ).start()
 
     def hail(semaphore, width):
         for dx in (-width, width):
@@ -386,6 +376,11 @@
             make_windows(x)
         for k in (0, 2, 3, 4, 5, 7):
             hand_out(k)
+
+        @pl.when(it > 0)
+        def _():
+            wait_sends(force_message, it - 1, 2 * it - 1)
+
         wait_arrivals(displacement_message, it, 2 * it, FAR)
         for x in (0, 9):
             make_windows(x)
@@ -396,8 +391,6 @@
         def _():
             hear(hail_four, 4)
             hail(hail_eight, 8)
-
-        wait_sends(displacement_message, it, 2 * it)
 
         live_below = jnp.where(it == 0, 2, 1)
 
@@ -515,6 +508,7 @@
         for i in range(2):
             fye[i] = edges([yr[1, i, c] for c in range(3)], other_edge_index)
         start(force_message, it, 2 * it + 1, NEAR)
+        wait_sends(displacement_message, it, 2 * it)
         wait_arrivals(force_message, it, 2 * it + 1, NEAR)
 
         lines = []
@@ -585,12 +579,14 @@
 
         @pl.when(it == ITERS - 1)
         def _():
-            first_sum.start()
+            sums = jnp.sum(sq[...], axis=1, keepdims=True)
+            row = jnp.sum(jnp.where(row8 == lane8, sums, 0.0), axis=0, keepdims=True)
+            total_row[...] = row
+            table[me] = row
+            send_squares()
 
         for x in (0, 7):
             update(x)
-        wait_sends(force_message, it, 2 * it + 1)
-
         @pl.when(it < ITERS - 1)
         def _():
             pack_far()
@@ -604,13 +600,14 @@
     lax.fori_loop(0, ITERS, iteration, 0)
     store_result = pltpu.make_async_copy(uc, uout, in_sem.at[0])
     store_result.start()
-    plane = first_sum.finish()
-    second_sum.source[...] = plane
-    second_sum.start()
-    total = second_sum.finish()
-    norms = jnp.sqrt(jnp.sum(total, axis=1, keepdims=True) / cells)
+    wait_sends(force_message, ITERS - 1, 2 * ITERS - 1)
+    others = table.at[0 : count - 1]
+    pltpu.make_async_copy(others, others, total_recv).wait()
+    pltpu.make_async_copy(others, others, total_send).wait()
+    total = jnp.sum(table[...], axis=0)
+    norms = jnp.sqrt(total / cells)
     for k in range(ITERS):
-        nout[k] = jnp.sum(norms[k : k + 1, :])
+        nout[k] = jnp.sum(norms[:, k : k + 1])
     store_result.wait()
 
 
@@ -672,18 +669,15 @@
                 v((3, tiles * 8, 128), F32),
                 v((8, 64, 384), F32),
                 v((8, 128), F32),
-                v((8, 128), F32),
-                v((2 * ny, 8, 128), F32),
-                v((nx, 8, 128), F32),
+                v((1, 128), F32),
+                v((2 * nx * ny, 1, 128), F32),
                 pltpu.SemaphoreType.REGULAR,
                 pltpu.SemaphoreType.REGULAR,
                 pltpu.SemaphoreType.DMA((6,)),
                 pltpu.SemaphoreType.DMA((2 * ITERS, 18)),
                 pltpu.SemaphoreType.DMA((2 * ITERS, 18)),
-                pltpu.SemaphoreType.DMA((2 * ny,)),
-                pltpu.SemaphoreType.DMA((2 * ny,)),
-                pltpu.SemaphoreType.DMA((nx,)),
-                pltpu.SemaphoreType.DMA((nx,)),
+                pltpu.SemaphoreType.DMA,
+                pltpu.SemaphoreType.DMA,
             ],
             compiler_params=pltpu.CompilerParams(
                 collective_id=0, has_side_effects=True, vmem_limit_bytes=24 * 2**20

time: 54.8 us -> 52.5 us (0.958)
  Pallas kernels: 52.9 us -> 50.6 us
    pallas_call x1, Pallas kernels: 52.9 us -> 50.6 us  [step(): pl.pallas_call(functools.partial(kernel, nx, ny, cells), out_shape=(jax.S...]
where the time goes in v4:
time: 52.5 us; the launch traced here: 52.4 us
  Pallas kernels  50.6 us (96%)
  local copies, waits for them, and re-layouts  1.15 us (2%)
  between operations  0.64 us (1%)
    pallas_call x1, Pallas kernels, step(): pl.pallas_call(functools.partial(kernel, nx, ny, cells), out_shape=(jax.S...  50.6 us
    unnamed x2, local copies, waits for them, and re-layouts  1.15 us

profile of v4, /device:TPU:1, one launch (start us, length us, event | category | flops | bytes accessed | tf_op | source)
XLA Modules:
  0.0 52.4 jit_solution(1409115067393063844)
XLA Ops:
  0.6 50.6 %relax.1 = (f32[3,8,8,128]{3,2,1,0:T(8,128)S(1)}, f32[3]{0:T(128)S(1)}) custom-call(s32[64]{0:T(128)} %tb_in.1, f32[3,8,8,128]{3,2,1,0:T(8,128)} %uold_in.1, f32[3,8,8,128]{3,2,1,0:T(8,128)} %utrial_in.1, f32[3,3,8,8,128]{4,3,2,1,0:T(8,128)} %jac_in.1, s32[4,64,128]{2,1,0:T(8,128)} %codes_in.1, s32[64,128]{1,0:T(8,128)} %groups_in.1), custom_call_target="tpu_custom_call" | custom-call | tf_op jit(solution)/shard_map/relax/pallas_call | solution.py:622
  51.3 0.6 %copy.10 = f32[3,8,8,128]{3,2,1,0:T(8,128)} copy(f32[3,8,8,128]{3,2,1,0:T(8,128)S(1)} %get-tuple-element.4) | data formatting | bytes 196608
  51.9 0.5 copy.11

commit v5 on v4

--- a/solution.py
+++ b/solution.py
@@ -53,7 +53,7 @@
     tb_ref, uold, jac, codes, groups, residuals,
     uc, uy, uxe, uye, ud, rxz, rxx, rxy, rxxe, rxye, rxd,
     pb, pz, yr, fxe, fye, fd, frz, frx, fry, frxe, frye, frd,
-    win, gat, kidx, lidx, geo, frozen, onehot, ohg, ohs, outs, acc,
+    win, gat, early, kidx, lidx, geo, frozen, onehot, ohg, ohs, outs, acc,
     sq, total_row, table,
     hail_four, hail_eight, in_sem, send_sem, recv_sem, total_send, total_recv,
 ):
@@ -372,10 +372,26 @@
             both = jnp.concatenate([win[k], win[k + 4]], axis=0)
             gat[k] = jnp.dot(pick, both, preferred_element_type=F32)
 
+        def look_up(n, at, planes, found):
+            ks = kidx[n, at, :]
+            ls = lidx[n, at, :]
+            for k in planes:
+                for c in range(3):
+                    value = take(gat[k, at, c * 128 : (c + 1) * 128], ls)
+                    found[c] = value if found[c] is None else jnp.where(ks == k, value, found[c])
+            return found
+
         for x in range(1, 9):
             make_windows(x)
         for k in (0, 2, 3, 4, 5, 7):
             hand_out(k)
+        for g in range(tiles // 8):
+            at = pl.ds(g * 8, 8)
+            for n in range(4):
+                planes = (0, 2, 3, 4, 5, 7) if n == 3 else (2, 3, 4, 5)
+                found = look_up(n, at, planes, [None] * 3)
+                for c in range(3):
+                    early[3 * n + c, at, :] = found[c]
 
         @pl.when(it > 0)
         def _():
@@ -398,15 +414,9 @@
             at = pl.ds(pl.multiple_of(g * 8, 8), 8)
             points = []
             for n in range(4):
-                ks = kidx[n, at, :]
-                ls = lidx[n, at, :]
-                least, most = ((2, 5), (1, 6), (1, 6), (0, 7))[n]
-                found = []
-                for c in range(3):
-                    value = take(gat[least, at, c * 128 : (c + 1) * 128], ls)
-                    for k in range(least + 1, most + 1):
-                        value = jnp.where(ks == k, take(gat[k, at, c * 128 : (c + 1) * 128], ls), value)
-                    found.append(value)
+                found = [early[3 * n + c, at, :] for c in range(3)]
+                if n > 0:
+                    found = look_up(n, at, (1, 6), found)
                 points.append(found)
             one = [points[1][c] - points[0][c] + geo[c, at, :] for c in range(3)]
             two = [points[3][c] - points[2][c] + geo[3 + c, at, :] for c in range(3)]
@@ -451,7 +461,7 @@
             spread_forces(g - 1, values)
             return later
 
-        values = lax.fori_loop(1, tiles // 8, group, pair_forces(0))
+        values = lax.fori_loop(1, tiles // 8, group, pair_forces(0), unroll=7)
         spread_forces(tiles // 8 - 1, values)
 
         def collect(k):
@@ -659,6 +669,7 @@
                 v((ITERS, 2, 2, 2, 8, 128), F32),
                 v((12, 64, 384), BF16),
                 v((8, tiles, 384), F32),
+                v((12, tiles, 128), F32),
                 v((4, tiles, 128), I32),
                 v((4, tiles, 128), I32),
                 v((9, tiles, 128), F32),

time: 52.5 us -> 49.6 us (0.945)
  Pallas kernels: 50.6 us -> 47.6 us
    pallas_call x1, Pallas kernels: 50.6 us -> 47.6 us  [step(): pl.pallas_call(functools.partial(kernel, nx, ny, cells), out_shape=(jax.S...]
where the time goes in v5:
time: 49.6 us; the launch traced here: 49.4 us
  Pallas kernels  47.6 us (96%)
  local copies, waits for them, and re-layouts  1.15 us (2%)
  between operations  0.64 us (1%)
    pallas_call x1, Pallas kernels, step(): pl.pallas_call(functools.partial(kernel, nx, ny, cells), out_shape=(jax.S...  47.6 us
    unnamed x2, local copies, waits for them, and re-layouts  1.15 us

profile of v5, /device:TPU:1, one launch (start us, length us, event | category | flops | bytes accessed | tf_op | source)
XLA Modules:
  0.0 49.4 jit_solution(9385524732675683247)
XLA Ops:
  0.6 47.6 %relax.1 = (f32[3,8,8,128]{3,2,1,0:T(8,128)S(1)}, f32[3]{0:T(128)S(1)}) custom-call(s32[64]{0:T(128)} %tb_in.1, f32[3,8,8,128]{3,2,1,0:T(8,128)} %uold_in.1, f32[3,8,8,128]{3,2,1,0:T(8,128)} %utrial_in.1, f32[3,3,8,8,128]{4,3,2,1,0:T(8,128)} %jac_in.1, s32[4,64,128]{2,1,0:T(8,128)} %codes_in.1, s32[64,128]{1,0:T(8,128)} %groups_in.1), custom_call_target="tpu_custom_call" | custom-call | tf_op jit(solution)/shard_map/relax/pallas_call | solution.py:632
  48.3 0.6 %copy.10 = f32[3,8,8,128]{3,2,1,0:T(8,128)} copy(f32[3,8,8,128]{3,2,1,0:T(8,128)S(1)} %get-tuple-element.4) | data formatting | bytes 196608
  48.9 0.5 %copy.11 = f32[3]{0:T(128)} copy(f32[3]{0:T(128)S(1)} %get-tuple-element.5) | data formatting | bytes 24

commit v6 on v5

--- a/solution.py
+++ b/solution.py
@@ -27,6 +27,10 @@
 
 FAR = [d for d in DIRS if d[0] != 0]
 NEAR = [d for d in DIRS if d[0] == 0]
+PACKED_FAR = [d for d in FAR if d[1] == 0 and d[2] == 1]
+PACKED_NEAR = [d for d in NEAR if d[1] != 0 and d[2] == 1]
+PLAIN_FAR = [d for d in FAR if d not in PACKED_FAR]
+PLAIN_NEAR = [d for d in NEAR if d not in PACKED_NEAR]
 
 
 def slot_of(dx, dy, z):
@@ -46,8 +50,17 @@
     return hi, x - hi
 
 
+def finish(cells, u, total, uout, nout, sem):
+    store = pltpu.make_async_copy(u, uout, sem)
+    store.start()
+    norms = jnp.sqrt(total[...] / cells)
+    for k in range(ITERS):
+        nout[k] = jnp.sum(norms[:, k : k + 1])
+    store.wait()
+
+
 def kernel(
-    nx, ny, cells,
+    nx, ny,
     tb_in, uold_in, utrial_in, jac_in, codes_in, groups_in,
     uout, nout,
     tb_ref, uold, jac, codes, groups, residuals,
@@ -178,24 +191,31 @@
     other_edge = 127 - my_edge
     my_edge_index = jnp.full((8, 128), my_edge, I32)
     other_edge_index = jnp.full((8, 128), other_edge, I32)
-    lane_index = [jnp.full((8, 128), c, I32) for c in range(3)]
+    column_lane = [row8 + 8 * c for c in range(3)]
 
     def edges(planes, index):
-        packed = take(planes[0], index)
-        for c in (1, 2):
-            packed = jnp.where(lane8 == c, take(planes[c], index), packed)
-        return packed
-
-    def pack_far():
+        packed = jnp.zeros((8, 128), F32)
+        for c in range(3):
+            packed = jnp.where(lane8 == column_lane[c], take(planes[c], index), packed)
+        return jnp.sum(packed, axis=0, keepdims=True)
+
+    def column(row, c):
+        return take(jnp.broadcast_to(row, (8, 128)), column_lane[c])
+
+    def corner_rows():
         for xi, x in ((0, 0), (1, 7)):
-            uxe[xi] = edges([uc[c, x] for c in range(3)], my_edge_index)
             for yi in range(2):
                 for c in range(3):
-                    ud[xi, yi, c : c + 1, :] = uy[yi, c, x : x + 1, :]
-
-    def pack_near():
-        for yi in range(2):
-            uye[yi] = edges([uy[yi, c] for c in range(3)], my_edge_index)
+                    ud[xi, yi, c] = uy[yi, c, x : x + 1, :]
+
+    def send_displacements(it, phase):
+        start(displacement_message, it, phase, PLAIN_FAR)
+        start(displacement_message, it, phase, PLAIN_NEAR)
+        for i in range(2):
+            uxe[i] = edges([uc[c, 7 * i] for c in range(3)], my_edge_index)
+            uye[i] = edges([uy[i, c] for c in range(3)], my_edge_index)
+        start(displacement_message, it, phase, PACKED_FAR)
+        start(displacement_message, it, phase, PACKED_NEAR)
 
     fetches[0].wait()
     for c in range(3):
@@ -203,12 +223,11 @@
             plane = uc[c, x]
             uy[0, c, x : x + 1, :] = plane[0:1]
             uy[1, c, x : x + 1, :] = plane[7:8]
-    pack_far()
-    pack_near()
+    corner_rows()
     beside_x = (gx > 0).astype(I32) + (gx < nx - 1).astype(I32)
     beside_y = (gy > 0).astype(I32) + (gy < ny - 1).astype(I32)
     pl.semaphore_wait(barrier, 2 * (1 + beside_x) * (1 + beside_y) - 1)
-    start(displacement_message, 0, 0, DIRS)
+    send_displacements(0, 0)
 
     for fetch in fetches[1:]:
         fetch.wait()
@@ -329,7 +348,7 @@
         wait_arrivals(displacement_message, it, 2 * it, NEAR)
 
         beyond_rows = [
-            [take(valid(y_ok[dy], rxye[it, lo_hi(dy)]), lane_index[c]) for c in range(3)] for dy in (-1, 1)
+            [column(valid(y_ok[dy], rxye[it, lo_hi(dy)]), c) for c in range(3)] for dy in (-1, 1)
         ]
         def make_windows(x):
             for c in range(3):
@@ -345,10 +364,10 @@
                 else:
                     dx, xi = (-1, 0) if x == 0 else (1, 1)
                     own = valid(x_ok[dx], rxx[it, xi, c])
-                    other = take(valid(x_ok[dx], rxxe[it, xi]), lane_index[c])
+                    other = column(valid(x_ok[dx], rxxe[it, xi]), c)
                     rows = [
                         [
-                            valid(exists(dx, dy), rxd[it, xi, lo_hi(dy), z, c : c + 1, :])
+                            valid(exists(dx, dy), rxd[it, xi, lo_hi(dy), z, c])
                             for z in (0, 1)
                         ]
                         for dy in (-1, 1)
@@ -502,22 +521,24 @@
                         if 1 <= x <= 8:
                             yr[z, yi, c, x - 1 : x, :] = ends[yi]
                         else:
-                            fd[z, 0 if x == 0 else 1, yi, c : c + 1, :] = ends[yi]
+                            fd[z, 0 if x == 0 else 1, yi, c] = ends[yi]
 
         for k in (1, 6):
             collect(k)
         for x in (0, 9):
             fold(x)
+        start(force_message, it, 2 * it + 1, PLAIN_FAR)
         for i in range(2):
             fxe[i] = edges([pz[c, 9 * i] for c in range(3)], other_edge_index)
-        start(force_message, it, 2 * it + 1, FAR)
+        start(force_message, it, 2 * it + 1, PACKED_FAR)
         for k in (0, 2, 3, 4, 5, 7):
             collect(k)
         for x in range(1, 9):
             fold(x)
+        start(force_message, it, 2 * it + 1, PLAIN_NEAR)
         for i in range(2):
             fye[i] = edges([yr[1, i, c] for c in range(3)], other_edge_index)
-        start(force_message, it, 2 * it + 1, NEAR)
+        start(force_message, it, 2 * it + 1, PACKED_NEAR)
         wait_sends(displacement_message, it, 2 * it)
         wait_arrivals(force_message, it, 2 * it + 1, NEAR)
 
@@ -528,7 +549,7 @@
                 [
                     valid(
                         y_ok[dy],
-                        fry[it, yi, c] + jnp.where(at_edge, take(frye[it, yi], lane_index[c]), 0.0),
+                        fry[it, yi, c] + jnp.where(at_edge, column(frye[it, yi], c), 0.0),
                     )
                     for c in range(3)
                 ]
@@ -541,7 +562,7 @@
                         xi = lo_hi(dx)
                         total = total + valid(
                             x_ok[dx],
-                            frx[it, xi, c] + jnp.where(at_edge, take(frxe[it, xi], lane_index[c]), 0.0),
+                            frx[it, xi, c] + jnp.where(at_edge, column(frxe[it, xi], c), 0.0),
                         )
                 for dy in (-1, 1):
                     yi = lo_hi(dy)
@@ -551,7 +572,7 @@
                             xi = lo_hi(dx)
                             line = line + valid(
                                 exists(dx, dy),
-                                frd[it, xi, yi, 0, c : c + 1, :] + frd[it, xi, yi, 1, c : c + 1, :],
+                                frd[it, xi, yi, 0, c] + frd[it, xi, yi, 1, c],
                             )
                     total = total + jnp.where(row8 == (0 if dy < 0 else 7), line, 0.0)
                 r = uc[c, x] - uold[c, x] - 0.5 * total
@@ -599,10 +620,8 @@
             update(x)
         @pl.when(it < ITERS - 1)
         def _():
-            pack_far()
-            start(displacement_message, it + 1, 2 * it + 2, FAR)
-            pack_near()
-            start(displacement_message, it + 1, 2 * it + 2, NEAR)
+            corner_rows()
+            send_displacements(it + 1, 2 * it + 2)
 
         return carry
 
@@ -614,10 +633,10 @@
     others = table.at[0 : count - 1]
     pltpu.make_async_copy(others, others, total_recv).wait()
     pltpu.make_async_copy(others, others, total_send).wait()
-    total = jnp.sum(table[...], axis=0)
-    norms = jnp.sqrt(total / cells)
-    for k in range(ITERS):
-        nout[k] = jnp.sum(norms[:, k : k + 1])
+    total_row[...] = jnp.sum(table[...], axis=0)
+    store_total = pltpu.make_async_copy(total_row, nout, in_sem.at[1])
+    store_total.start()
+    store_total.wait()
     store_result.wait()
 
 
@@ -629,14 +648,14 @@
         cells = float(3 * 8 * 8 * 128 * nx * ny * mesh.shape["gz"])
         smem = pl.BlockSpec(memory_space=pltpu.SMEM)
         v = pltpu.VMEM
-        return pl.pallas_call(
-            functools.partial(kernel, nx, ny, cells),
+        u_final, total = pl.pallas_call(
+            functools.partial(kernel, nx, ny),
             out_shape=(
                 jax.ShapeDtypeStruct(u_old.shape, F32),
-                jax.ShapeDtypeStruct((ITERS,), F32),
+                jax.ShapeDtypeStruct((1, 128), F32),
             ),
             in_specs=[pl.BlockSpec(memory_space=pltpu.HBM)] * 6,
-            out_specs=(pl.BlockSpec(memory_space=pl.ANY), smem),
+            out_specs=[pl.BlockSpec(memory_space=pl.ANY)] * 2,
             scratch_shapes=[
                 pltpu.SMEM(tile_base.shape, I32),
                 v(u_old.shape, F32),
@@ -646,27 +665,27 @@
                 v(u_old.shape, F32),
                 v((3, 8, 8, 128), F32),
                 v((2, 3, 8, 128), F32),
-                v((2, 8, 128), F32),
-                v((2, 8, 128), F32),
-                v((2, 2, 8, 128), F32),
+                v((2, 1, 128), F32),
+                v((2, 1, 128), F32),
+                v((2, 2, 3, 1, 128), F32),
                 v((ITERS, 3, 8, 8, 128), F32),
                 v((ITERS, 2, 3, 8, 128), F32),
                 v((ITERS, 2, 3, 8, 128), F32),
-                v((ITERS, 2, 8, 128), F32),
-                v((ITERS, 2, 8, 128), F32),
-                v((ITERS, 2, 2, 2, 8, 128), F32),
+                v((ITERS, 2, 1, 128), F32),
+                v((ITERS, 2, 1, 128), F32),
+                v((ITERS, 2, 2, 2, 3, 1, 128), F32),
                 v((3, 10, 8, 128), F32),
                 v((3, 10, 8, 128), F32),
                 v((2, 2, 3, 8, 128), F32),
-                v((2, 8, 128), F32),
-                v((2, 8, 128), F32),
-                v((2, 2, 2, 8, 128), F32),
+                v((2, 1, 128), F32),
+                v((2, 1, 128), F32),
+                v((2, 2, 2, 3, 1, 128), F32),
                 v((ITERS, 3, 8, 8, 128), F32),
                 v((ITERS, 2, 3, 8, 128), F32),
                 v((ITERS, 2, 3, 8, 128), F32),
-                v((ITERS, 2, 8, 128), F32),
-                v((ITERS, 2, 8, 128), F32),
-                v((ITERS, 2, 2, 2, 8, 128), F32),
+                v((ITERS, 2, 1, 128), F32),
+                v((ITERS, 2, 1, 128), F32),
+                v((ITERS, 2, 2, 2, 3, 1, 128), F32),
                 v((12, 64, 384), BF16),
                 v((8, tiles, 384), F32),
                 v((12, tiles, 128), F32),
@@ -700,6 +719,18 @@
                 for a in (tile_base, u_old, u_trial, jacobian_inverse, pair_codes, pair_groups)
             )
         )
+        return pl.pallas_call(
+            functools.partial(finish, cells),
+            out_shape=(
+                jax.ShapeDtypeStruct(u_old.shape, F32),
+                jax.ShapeDtypeStruct((ITERS,), F32),
+            ),
+            in_specs=[pl.BlockSpec(memory_space=pl.ANY), pl.BlockSpec(memory_space=pltpu.VMEM)],
+            out_specs=(pl.BlockSpec(memory_space=pl.ANY), smem),
+            scratch_shapes=[pltpu.SemaphoreType.DMA],
+            compiler_params=pltpu.CompilerParams(vmem_limit_bytes=2**20),
+            name="finish",
+        )(u_final, total)
 
     everywhere = ("gx", "gy", "gz")
     return jax.shard_map(

time: 49.6 us -> 48.2 us (0.972)
  local copies, waits for them, and re-layouts: 1.15 us -> 0 us
    unnamed x2 -> x0, local copies, waits for them, and re-layouts: 1.15 us -> none
    pallas_call x1 -> x2, Pallas kernels: 47.6 us -> 47.4 us  [the longest x1 46.3 us: step(): pl.pallas_call(functools.partial(kernel, nx, ny), out_shape=(jax.ShapeDty...]
where the time goes in v6:
time: 48.2 us; the launch traced here: 48.1 us
  Pallas kernels  47.4 us (98%)
  between operations  0.64 us (1%)
    pallas_call x1, Pallas kernels, step(): pl.pallas_call(functools.partial(kernel, nx, ny), out_shape=(jax.ShapeDty...  46.3 us
    pallas_call x1, Pallas kernels, step(): pl.pallas_call(functools.partial(finish, cells), out_shape=(jax.ShapeDtyp...  1.17 us

profile of v6, /device:TPU:1, one launch (start us, length us, event | category | flops | bytes accessed | tf_op | source)
XLA Modules:
  0.0 48.1 jit_solution(13746041480030059912)
XLA Ops:
  0.6 46.3 %relax.1 = (f32[3,8,8,128]{3,2,1,0:T(8,128)S(1)}, f32[1,128]{1,0:T(1,128)S(1)}) custom-call(s32[64]{0:T(128)} %tb_in.1, f32[3,8,8,128]{3,2,1,0:T(8,128)} %uold_in.1, f32[3,8,8,128]{3,2,1,0:T(8,128)} %utrial_in.1, f32[3,3,8,8,128]{4,3,2,1,0:T(8,128)} %jac_in.1, s32[4,64,128]{2,1,0:T(8,128)} %codes_in.1, s32[64,128]{1,0:T(8,128)} %groups_in.1), custom_call_target="tpu_custom_call" | custom-call | tf_op jit(solution)/shard_map/relax/pallas_call | solution.py:651
  46.9 1.2 %finish.1 = (f32[3,8,8,128]{3,2,1,0:T(8,128)}, f32[3]{0:T(128)}) custom-call(f32[3,8,8,128]{3,2,1,0:T(8,128)S(1)} %get-tuple-element.4.u, f32[1,128]{1,0:T(1,128)S(1)} %get-tuple-element.5.total), custom_call_target="tpu_custom_call" | custom-call | tf_op jit(solution)/shard_map/finish/pallas_call | solution.py:722
